TPU v7x, 32 devices: a whole 2x2x4 slice. The times are simulated.
32 devices in a mesh: row: 8 (over y, x, core), col: 4 (over z).
Axes of the slice: x: 2, y: 2, z: 4, core: 2. Of those that a mesh axis runs over, the one named last changes fastest.
Arguments:
- density: float32 [256, 256, 256], P('row', 'col'), may hold values from -5 to 5
- green_octant: float32 [256, 256, 256], P('row', 'col'), may hold values from 0 to 0.25
Outputs:
- potential: float32 [256, 256, 256], P('row', 'col')
All inputs are finite; a program needn't handle non-finite values.
Results may differ from a plain program's by a relative error of at most 0.000092.
Values sent between devices are 32-bit elements; how exact they have to be, the bound alone decides.
No kernel may reach another device: no remote copies, remote signals or barrier semaphores. Data moves between devices by JAX's collectives and lax.ppermute only.
A program may use at most 192 MiB of HBM per device.

v0:
```python
import jax
import jax.numpy as jnp
from jax import lax
from jax.sharding import PartitionSpec as P


def tables(extent, padded):
    positions = lax.iota(jnp.int32, extent)[:, None]
    waves = lax.iota(jnp.int32, padded)[None, :]
    phases = positions * waves % padded
    angles = phases.astype(jnp.float32) * jnp.float32(2.0 * 3.141592653589793 / padded)
    weights = jnp.where(positions == 0, jnp.float32(1.0), jnp.float32(2.0))
    cosine = jnp.cos(angles)
    return (cosine, jnp.sin(angles), weights * cosine)


def contract(pattern, operand, matrix):
    return jnp.einsum(
        pattern,
        operand,
        matrix,
        precision=lax.Precision.HIGHEST,
        preferred_element_type=jnp.float32,
    )


def forward(pattern, real_part, imaginary, kernel, cosine, sine_table, kernel_table):
    new_real = contract(pattern, real_part, cosine) + contract(pattern, imaginary, sine_table)
    new_imaginary = contract(pattern, imaginary, cosine) - contract(pattern, real_part, sine_table)
    return (new_real, new_imaginary, contract(pattern, kernel, kernel_table))


def inverse(pattern, real_part, imaginary, cosine, sine_table):
    new_real = contract(pattern, real_part, cosine) - contract(pattern, imaginary, sine_table)
    new_imaginary = contract(pattern, imaginary, cosine) + contract(pattern, real_part, sine_table)
    return (new_real, new_imaginary)


def nyquist_plane(density, green_octant, cosine, sine_table, kernel_table):
    extent = density.shape[2]
    local_cols = density.shape[1]
    alternating = cosine[:, extent]
    dens_line = contract("xyz,z->xy", density, alternating)
    kern_line = contract("xyz,z->xy", green_octant, kernel_table[:, extent])
    dens_line, kern_line = (
        lax.all_gather(dens_line, "col", axis=1, tiled=True),
        lax.all_gather(kern_line, "col", axis=1, tiled=True),
    )
    real_part = contract("xy,yq->xq", dens_line, cosine)
    imaginary = -contract("xy,yq->xq", dens_line, sine_table)
    kernel = contract("xy,yq->xq", kern_line, kernel_table)
    real_part, imaginary, kernel = (
        lax.all_to_all(real_part, "row", split_axis=1, concat_axis=0, tiled=True),
        lax.all_to_all(imaginary, "row", split_axis=1, concat_axis=0, tiled=True),
        lax.all_to_all(kernel, "row", split_axis=1, concat_axis=0, tiled=True),
    )
    real_part, imaginary, kernel = forward(
        "xq,xp->pq", real_part, imaginary, kernel, cosine, sine_table, kernel_table
    )
    real_part = real_part * kernel
    imaginary = imaginary * kernel
    real_part, imaginary = inverse("pq,xp->xq", real_part, imaginary, cosine, sine_table)
    real_part, imaginary = (
        lax.all_to_all(real_part, "row", split_axis=0, concat_axis=1, tiled=True),
        lax.all_to_all(imaginary, "row", split_axis=0, concat_axis=1, tiled=True),
    )
    whole = contract("xq,yq->xy", real_part, cosine) - contract("xq,yq->xy", imaginary, sine_table)
    start = lax.axis_index("col") * local_cols
    return lax.dynamic_slice_in_dim(whole, start, local_cols, 1)


def on_device(density, green_octant):
    extent = density.shape[2]
    padded = 2 * extent
    cosine, sine_table, kernel_table = tables(extent, padded)
    half_cos = cosine[:, :extent]
    half_sin = sine_table[:, :extent]
    real_part = contract("xyz,zk->xyk", density, half_cos)
    imaginary = -contract("xyz,zk->xyk", density, half_sin)
    kernel = contract("xyz,zk->xyk", green_octant, kernel_table[:, :extent])
    real_part, imaginary, kernel = (
        lax.all_to_all(real_part, "col", split_axis=2, concat_axis=1, tiled=True),
        lax.all_to_all(imaginary, "col", split_axis=2, concat_axis=1, tiled=True),
        lax.all_to_all(kernel, "col", split_axis=2, concat_axis=1, tiled=True),
    )
    real_part, imaginary, kernel = forward(
        "xyk,yq->xqk", real_part, imaginary, kernel, cosine, sine_table, kernel_table
    )
    real_part, imaginary, kernel = (
        lax.all_to_all(real_part, "row", split_axis=1, concat_axis=0, tiled=True),
        lax.all_to_all(imaginary, "row", split_axis=1, concat_axis=0, tiled=True),
        lax.all_to_all(kernel, "row", split_axis=1, concat_axis=0, tiled=True),
    )
    real_part, imaginary, kernel = forward(
        "xqk,xp->pqk", real_part, imaginary, kernel, cosine, sine_table, kernel_table
    )
    real_part = real_part * kernel
    imaginary = imaginary * kernel
    real_part, imaginary = inverse("pqk,xp->xqk", real_part, imaginary, cosine, sine_table)
    real_part, imaginary = (
        lax.all_to_all(real_part, "row", split_axis=0, concat_axis=1, tiled=True),
        lax.all_to_all(imaginary, "row", split_axis=0, concat_axis=1, tiled=True),
    )
    real_part, imaginary = inverse("xqk,yq->xyk", real_part, imaginary, cosine, sine_table)
    real_part, imaginary = (
        lax.all_to_all(real_part, "col", split_axis=1, concat_axis=2, tiled=True),
        lax.all_to_all(imaginary, "col", split_axis=1, concat_axis=2, tiled=True),
    )
    highest = nyquist_plane(density, green_octant, cosine, sine_table, kernel_table)
    waves = lax.iota(jnp.int32, extent)[None, :]
    doubling = jnp.where(waves == 0, jnp.float32(1.0), jnp.float32(2.0))
    summed = contract("xyk,zk->xyz", real_part, half_cos * doubling) - contract(
        "xyk,zk->xyz", imaginary, half_sin * doubling
    )
    summed = summed + highest[:, :, None] * cosine[:, extent][None, None, :]
    scaling = 1.0 / float(padded * padded * padded)
    return summed * jnp.float32(scaling)


def solution(mesh):
    return jax.shard_map(
        on_device,
        mesh=mesh,
        in_specs=(P("row", "col", None), P("row", "col", None)),
        out_specs=P("row", "col", None),
        check_vma=False,
    )
```

profile of v0, /device:TPU:1, one launch (start us, length us, event | category | flops | bytes accessed | tf_op | source)
XLA Modules:
  0.0 1006.5 jit_solution(2282553187442278310)
XLA Ops:
  38.4 31.7 %all-to-all-done.1 = f32[4,1,131072]{2,1,0:T(1,128)} async-done(((f32[4,1,131072]{2,1,0:T(1,128)}), f32[4,1,131072]{2,1,0:T(1,128)}, u32[]{:S(2)}, u32[]{:S(2)}) %all-to-all-start.1) | async-done | bytes 2097184 | tf_op jit(solution)/shard_map/all_to_all | solution.py:83
  92.6 30.1 %all-to-all-done = f32[4,1,131072]{2,1,0:T(1,128)} async-done(((f32[4,1,131072]{2,1,0:T(1,128)}), f32[4,1,131072]{2,1,0:T(1,128)}, u32[]{:S(2)}, u32[]{:S(2)}) %all-to-all-start) | async-done | bytes 2097184 | tf_op jit(solution)/shard_map/all_to_all | solution.py:82
  149.1 13.8 %all_to_all.207 = f32[32,256,64]{1,2,0:T(8,128)} reshape(f32[32,4,64,64]{2,1,3,0:T(4,128)} %bitcast.280) | data formatting | bytes 4194304 | tf_op jit(solution)/shard_map/all_to_all | solution.py:83
  215.4 9.8 reshape.93
  256.6 9.8 reshape.95
  266.4 10.3 %all-to-all-done.2 = f32[8,1,131072]{2,1,0:T(1,128)} async-done(((f32[8,1,131072]{2,1,0:T(1,128)}), f32[8,1,131072]{2,1,0:T(1,128)}, u32[]{:S(2)}, u32[]{:S(2)}) %all-to-all-start.2) | async-done | bytes 4194336 | tf_op jit(solution)/shard_map/all_to_all | solution.py:90
  329.5 9.8 reshape.87
  346.5 10.9 %all-gather = f32[4,64,32]{1,2,0:T(8,128)S(1)} all-gather(f32[1,64,32]{1,2,0:T(8,128)S(1)} %bitcast.308), channel_id=1, replica_groups=mesh['row'=8,'col'=4] {'col'}, dimensions={0}, use_global_device_ids=true | all-gather | bytes 40960 | tf_op jit(solution)/shard_map/all_gather | solution.py:46
  367.2 10.3 %all-gather.1 = f32[4,64,32]{1,2,0:T(8,128)S(1)} all-gather(f32[1,64,32]{1,2,0:T(8,128)S(1)} %bitcast.307), channel_id=1, replica_groups=mesh['row'=8,'col'=4] {'col'}, dimensions={0}, use_global_device_ids=true | all-gather | bytes 40960 | tf_op jit(solution)/shard_map/all_gather | solution.py:47
  380.9 13.9 %reduce.10 = f32[8,131072]{1,0:T(8,128)} reduce(f32[8,1,131072]{2,1,0:T(1,128)} %all-to-all-done.2, f32[]{:T(128)} %broadcast.80), dimensions={1}, to_apply=%all_to_all.208.reduce_sub_computation | reduce | bytes 8388612 | tf_op jit(solution)/shard_map/all_to_all | solution.py:90
  403.4 11.3 %copy.42 = f32[32,8,64,64]{3,2,0,1:T(8,128)} copy(f32[32,8,64,64]{3,0,2,1:T(8,128)} %bitcast.253) | data formatting | bytes 8388608 | tf_op jit(solution)/shard_map/all_to_all | solution.py:90
  422.5 14.1 %reduce.9 = f32[8,131072]{1,0:T(8,128)} reduce(f32[8,1,131072]{2,1,0:T(1,128)} %all-to-all-done.3, f32[]{:T(128)} %broadcast.80), dimensions={1}, to_apply=%all_to_all.212.reduce_sub_computation | reduce | bytes 8388612 | tf_op jit(solution)/shard_map/all_to_all | solution.py:91
  445.3 11.3 %copy.45 = f32[32,8,64,64]{3,2,0,1:T(8,128)} copy(f32[32,8,64,64]{3,0,2,1:T(8,128)} %bitcast.255) | data formatting | bytes 8388608 | tf_op jit(solution)/shard_map/all_to_all | solution.py:91
  464.4 14.8 %fusion.35 = f32[512,4096]{0,1} fusion(f32[256,4096]{0,1:T(8,128)} %bitcast.239), kind=kOutput, calls=%fused_computation.51 | convolution fusion | flops 6444285952 | bytes 12582912
  479.2 13.0 %fusion.62 = f32[512,4096]{0,1} fusion(f32[256,4096]{0,1:T(8,128)S(1)} %bitcast.240), kind=kOutput, calls=%fused_computation.62 | convolution fusion | flops 6444285952 | bytes 12582912
  492.2 13.2 %fusion.60 = f32[512,4096]{0,1} fusion(f32[256,4096]{0,1:T(8,128)S(1)} %bitcast.237), kind=kOutput, calls=%fused_computation.61 | convolution fusion | flops 6444285952 | bytes 12582912
  505.3 12.9 %fusion.41 = f32[512,4096]{0,1} fusion(f32[256,4096]{0,1:T(8,128)S(1)} %bitcast.238), kind=kOutput, calls=%fused_computation.54 | convolution fusion | flops 6444285952 | bytes 12582912
  518.2 10.5 %all-to-all-start.11 = ((f32[8,1,2048]{2,1,0:T(1,128)}), f32[8,1,2048]{2,1,0:T(1,128)S(1)}, u32[]{:S(2)}, u32[]{:S(2)}) async-start(f32[8,1,2048]{2,1,0:T(1,128)} %reshape.107), calls=%async_computation.11 | async-start | bytes 131072 | tf_op jit(solution)/shard_map/all_to_all | solution.py:54
  528.8 13.6 %reduce.6 = f32[8,131072]{1,0:T(8,128)} reduce(f32[8,1,131072]{2,1,0:T(1,128)} %all-to-all-done.5, f32[]{:T(128)} %broadcast.80), dimensions={1}, to_apply=%all_to_all.220.reduce_sub_computation | reduce | bytes 8388612 | tf_op jit(solution)/shard_map/all_to_all | solution.py:92
  551.1 11.3 %copy.50 = f32[32,8,64,64]{3,2,0,1:T(8,128)} copy(f32[32,8,64,64]{3,0,2,1:T(8,128)} %bitcast.257) | data formatting | bytes 8388608 | tf_op jit(solution)/shard_map/all_to_all | solution.py:92
  570.1 14.6 %fusion.70 = f32[512,4096]{0,1} fusion(f32[256,4096]{0,1:T(8,128)} %bitcast.270, f32[256]{0:T(256)S(1)} %compare_select_fusion), kind=kOutput, calls=%fused_computation.67 | convolution fusion | flops 6444417024 | bytes 12583936
  584.7 22.7 %subtract_multiply_fusion = (f32[512,64,64]{0,2,1:T(8,128)}, f32[512,64,64]{0,2,1:T(8,128)}) fusion(f32[512,64,64]{0,2,1:T(8,128)} %bitcast.249, f32[512,64,64]{0,2,1:T(8,128)} %bitcast.245, f32[512,64,64]{0,2,1:T(8,128)} %bitcast.247, f32[512,64,64]{0,2,1:T(8,128)} %bitcast.248, f32[512,64,64]{0,2,1:T(8,128)} %bitcast.246), kind=kLoop, calls=%fused_computation | loop fusion | flops 8388608 | bytes 58720256 | tf_op jit(solution)/shard_map/mul | solution.py:98
  611.6 14.1 %fusion.56 = f32[256,4096]{0,1} fusion(f32[512,4096]{0,1:T(8,128)} %bitcast.235), kind=kOutput, calls=%fused_computation.59 | convolution fusion | flops 6444285952 | bytes 12582912
  630.2 13.6 %fusion.31 = f32[256,4096]{0,1:S(1)} fusion(f32[512,4096]{0,1:T(8,128)} %bitcast.233), kind=kOutput, calls=%fused_computation.49 | convolution fusion | flops 6444285952 | bytes 12582912
  655.7 9.8 reshape.99
  670.5 13.4 %fusion.37 = f32[256,4096]{0,1:S(1)} fusion(f32[512,4096]{0,1:T(8,128)} %bitcast.236), kind=kOutput, calls=%fused_computation.52 | convolution fusion | flops 6444285952 | bytes 12582912
  683.9 13.3 %fusion.58 = f32[256,4096]{0,1:S(1)} fusion(f32[512,4096]{0,1:T(8,128)} %bitcast.234), kind=kOutput, calls=%fused_computation.60 | convolution fusion | flops 6444285952 | bytes 12582912
  709.4 9.8 reshape.97
  751.5 14.1 %reduce.12 = f32[8,131072]{1,0:T(8,128)} reduce(f32[8,1,131072]{2,1,0:T(1,128)} %all-to-all-done.7, f32[]{:T(128)} %broadcast.80), dimensions={1}, to_apply=%all_to_all.228.reduce_sub_computation | reduce | bytes 8388612 | tf_op jit(solution)/shard_map/all_to_all | solution.py:102
  803.1 13.7 %reduce.11 = f32[8,131072]{1,0:T(8,128)} reduce(f32[8,1,131072]{2,1,0:T(1,128)} %all-to-all-done.6, f32[]{:T(128)} %broadcast.80), dimensions={1}, to_apply=%all_to_all.224.reduce_sub_computation | reduce | bytes 8388612 | tf_op jit(solution)/shard_map/all_to_all | solution.py:101
  900.7 22.1 %all-to-all-done.9 = f32[4,1,131072]{2,1,0:T(1,128)} async-done(((f32[4,1,131072]{2,1,0:T(1,128)}), f32[4,1,131072]{2,1,0:T(1,128)}, u32[]{:S(2)}, u32[]{:S(2)}) %all-to-all-start.9) | async-done | bytes 2097184 | tf_op jit(solution)/shard_map/all_to_all | solution.py:107
  958.6 16.4 %all-to-all-done.8 = f32[4,1,131072]{2,1,0:T(1,128)} async-done(((f32[4,1,131072]{2,1,0:T(1,128)}), f32[4,1,131072]{2,1,0:T(1,128)}, u32[]{:S(2)}, u32[]{:S(2)}) %all-to-all-start.8) | async-done | bytes 2097184 | tf_op jit(solution)/shard_map/all_to_all | solution.py:106
  (177 shorter events, 551.5 us)
Async XLA Ops:
  0.0 2.7 copy-start
  1.9 0.8 copy-start.12
  16.9 53.3 %all-to-all-start.1 = ((f32[4,1,131072]{2,1,0:T(1,128)}), f32[4,1,131072]{2,1,0:T(1,128)}, u32[]{:S(2)}, u32[]{:S(2)}) async-start(f32[4,1,131072]{2,1,0:T(1,128)} %reshape.91), calls=%async_computation.1 | async-start | bytes 4194304 | tf_op jit(solution)/shard_map/all_to_all | solution.py:83
  24.2 319.6 %copy-start.10 = (f32[256,512]{1,0:T(8,128)}, f32[256,512]{1,0:T(8,128)S(1)}, u32[]{:S(2)}) copy-start(f32[256,512]{1,0:T(8,128)S(1)} %fusion.16) | copy-start | bytes 1572868
  70.2 52.6 %all-to-all-start = ((f32[4,1,131072]{2,1,0:T(1,128)}), f32[4,1,131072]{2,1,0:T(1,128)}, u32[]{:S(2)}, u32[]{:S(2)}) async-start(f32[4,1,131072]{2,1,0:T(1,128)} %reshape.89), calls=%async_computation | async-start | bytes 4194304 | tf_op jit(solution)/shard_map/all_to_all | solution.py:82
  122.8 102.5 %all-to-all-start.4 = ((f32[4,1,131072]{2,1,0:T(1,128)}), f32[4,1,131072]{2,1,0:T(1,128)}, u32[]{:S(2)}, u32[]{:S(2)}) async-start(f32[4,1,131072]{2,1,0:T(1,128)} %reshape.85), calls=%async_computation.4 | async-start | bytes 4194304 | tf_op jit(solution)/shard_map/all_to_all | solution.py:84
  189.9 7.4 copy-start.5
  225.2 51.5 %all-to-all-start.2 = ((f32[8,1,131072]{2,1,0:T(1,128)}), f32[8,1,131072]{2,1,0:T(1,128)}, u32[]{:S(2)}, u32[]{:S(2)}) async-start(f32[8,1,131072]{2,1,0:T(1,128)} %reshape.93), calls=%async_computation.2 | async-start | bytes 8388608 | tf_op jit(solution)/shard_map/all_to_all | solution.py:90
  231.1 7.5 copy-start.6
  276.7 62.6 %all-to-all-start.3 = ((f32[8,1,131072]{2,1,0:T(1,128)}), f32[8,1,131072]{2,1,0:T(1,128)}, u32[]{:S(2)}, u32[]{:S(2)}) async-start(f32[8,1,131072]{2,1,0:T(1,128)} %reshape.95), calls=%async_computation.3 | async-start | bytes 8388608 | tf_op jit(solution)/shard_map/all_to_all | solution.py:91
  339.3 179.0 %all-to-all-start.5 = ((f32[8,1,131072]{2,1,0:T(1,128)}), f32[8,1,131072]{2,1,0:T(1,128)}, u32[]{:S(2)}, u32[]{:S(2)}) async-start(f32[8,1,131072]{2,1,0:T(1,128)} %reshape.87), calls=%async_computation.5 | async-start | bytes 8388608 | tf_op jit(solution)/shard_map/all_to_all | solution.py:92
  344.0 13.5 %copy-start.14 = (f32[256]{0:T(256)}, f32[256]{0:T(256)S(1)}, u32[]{:S(2)}) copy-start(f32[256]{0:T(256)S(1)} %slice_reduce_fusion.1) | copy-start | bytes 3076
  346.5 18.0 %copy-start.9 = (f32[32,64,256]{2,1,0:T(8,128)S(1)}, f32[32,64,256]{2,1,0:T(8,128)}, u32[]{:S(2)}) copy-start(f32[32,64,256]{2,1,0:T(8,128)} %param.3) | copy-start | bytes 6291460
  464.4 14.8 %copy-start.3 = (f32[256,64,64]{0,2,1:T(8,128)S(1)}, f32[256,64,64]{0,2,1:T(8,128)}, u32[]{:S(2)}) copy-start(f32[256,64,64]{0,2,1:T(8,128)} %copy.46) | copy-start | bytes 12582916
  479.2 13.0 %copy-start.2 = (f32[256,64,64]{0,2,1:T(8,128)S(1)}, f32[256,64,64]{0,2,1:T(8,128)}, u32[]{:S(2)}) copy-start(f32[256,64,64]{0,2,1:T(8,128)} %copy.43) | copy-start | bytes 12582916
  518.2 89.1 %all-to-all-start.11 = ((f32[8,1,2048]{2,1,0:T(1,128)}), f32[8,1,2048]{2,1,0:T(1,128)S(1)}, u32[]{:S(2)}, u32[]{:S(2)}) async-start(f32[8,1,2048]{2,1,0:T(1,128)} %reshape.107), calls=%async_computation.11 | async-start | bytes 131072 | tf_op jit(solution)/shard_map/all_to_all | solution.py:54
  607.4 18.3 %all-to-all-start.10 = ((f32[8,1,2048]{2,1,0:T(1,128)}), f32[8,1,2048]{2,1,0:T(1,128)S(1)}, u32[]{:S(2)}, u32[]{:S(2)}) async-start(f32[8,1,2048]{2,1,0:T(1,128)} %reshape.109), calls=%async_computation.10 | async-start | bytes 131072 | tf_op jit(solution)/shard_map/all_to_all | solution.py:53
  625.7 39.9 %all-to-all-start.12 = ((f32[8,1,2048]{2,1,0:T(1,128)}), f32[8,1,2048]{2,1,0:T(1,128)S(1)}, u32[]{:S(2)}, u32[]{:S(2)}) async-start(f32[8,1,2048]{2,1,0:T(1,128)} %reshape.105), calls=%async_computation.12 | async-start | bytes 131072 | tf_op jit(solution)/shard_map/all_to_all | solution.py:55
  630.1 13.6 %copy-start.7 = (f32[256,4096]{0,1:S(1)}, f32[256,4096]{0,1}, u32[]{:S(2)}) copy-start(f32[256,4096]{0,1} %fusion.56) | copy-start | bytes 12582916
  665.6 53.7 %all-to-all-start.7 = ((f32[8,1,131072]{2,1,0:T(1,128)}), f32[8,1,131072]{2,1,0:T(1,128)}, u32[]{:S(2)}, u32[]{:S(2)}) async-start(f32[8,1,131072]{2,1,0:T(1,128)} %reshape.99), calls=%async_computation.7 | async-start | bytes 8388608 | tf_op jit(solution)/shard_map/all_to_all | solution.py:102
  719.3 79.4 %all-to-all-start.6 = ((f32[8,1,131072]{2,1,0:T(1,128)}), f32[8,1,131072]{2,1,0:T(1,128)}, u32[]{:S(2)}, u32[]{:S(2)}) async-start(f32[8,1,131072]{2,1,0:T(1,128)} %reshape.97), calls=%async_computation.6 | async-start | bytes 8388608 | tf_op jit(solution)/shard_map/all_to_all | solution.py:101
  798.6 52.4 %all-to-all-start.14 = ((f32[8,1,2048]{2,1,0:T(1,128)}), f32[8,1,2048]{2,1,0:T(1,128)S(1)}, u32[]{:S(2)}, u32[]{:S(2)}) async-start(f32[8,1,2048]{2,1,0:T(1,128)} %reshape.111), calls=%async_computation.14 | async-start | bytes 131072 | tf_op jit(solution)/shard_map/all_to_all | solution.py:65
  851.0 19.0 %all-to-all-start.13 = ((f32[8,1,2048]{2,1,0:T(1,128)}), f32[8,1,2048]{2,1,0:T(1,128)S(1)}, u32[]{:S(2)}, u32[]{:S(2)}) async-start(f32[8,1,2048]{2,1,0:T(1,128)} %reshape.113), calls=%async_computation.13 | async-start | bytes 131072 | tf_op jit(solution)/shard_map/all_to_all | solution.py:64
  870.0 52.7 %all-to-all-start.9 = ((f32[4,1,131072]{2,1,0:T(1,128)}), f32[4,1,131072]{2,1,0:T(1,128)}, u32[]{:S(2)}, u32[]{:S(2)}) async-start(f32[4,1,131072]{2,1,0:T(1,128)} %reshape.103), calls=%async_computation.9 | async-start | bytes 4194304 | tf_op jit(solution)/shard_map/all_to_all | solution.py:107
  874.5 7.6 copy-start.4
  922.7 52.3 %all-to-all-start.8 = ((f32[4,1,131072]{2,1,0:T(1,128)}), f32[4,1,131072]{2,1,0:T(1,128)}, u32[]{:S(2)}, u32[]{:S(2)}) async-start(f32[4,1,131072]{2,1,0:T(1,128)} %reshape.101), calls=%async_computation.8 | async-start | bytes 4194304 | tf_op jit(solution)/shard_map/all_to_all | solution.py:106
  993.5 5.6 copy-start.11
  993.5 9.3 copy-start.13
  993.5 9.3 copy-start.15
  999.1 3.7 copy-start.8
  999.1 7.0 copy-start.1
where the time goes:
time: 1020 us; the launch traced here: 1010 us
  local copies, waits for them, and re-layouts  386 us (38%)
  matrix products  246 us (24%)
  other arithmetic  162 us (16%)
  waiting for transfers between devices  111 us (11%)
  starting transfers between devices  80.1 us (8%)
  blocking collectives  21.2 us (2%)
    unnamed x18, matrix products  187 us
    unnamed x64, local copies, waits for them, and re-layouts  150 us
    dot_general x21, matrix products, contract(): jnp.einsum(pattern, operand, matrix, precision=lax.Precision.HIGHEST, pre...  58.9 us
    all_to_all x1, waiting for transfers between devices, on_device(): lax.all_to_all(imaginary, 'col', split_axis=2, concat_axis=1, tiled=True)  31.7 us
    all_to_all x1, waiting for transfers between devices, on_device(): lax.all_to_all(real_part, 'col', split_axis=2, concat_axis=1, tiled=True)  30.1 us
    mul x1, other arithmetic, on_device(): imaginary = imaginary * kernel  22.7 us
    all_to_all x1, waiting for transfers between devices, on_device(): lax.all_to_all(imaginary, 'col', split_axis=1, concat_axis=2, tiled=True)  22.1 us
    all_to_all x2, local copies, waits for them, and re-layouts, on_device(): lax.all_to_all(imaginary, 'col', split_axis=2, concat_axis=1, tiled=True)  20.7 us
  transfers between devices with their start and end apart: 15, of which 5 were waited for; matrix products, arithmetic and copies ran while one was open for 70% of the time, Pallas kernels for 0%

commit v1 on v0

v1 whole, which is shorter than its diff:
```python
import numpy as np
import jax
import jax.numpy as jnp
from jax import lax
from jax.experimental import pallas as pl
from jax.experimental.pallas import tpu as pltpu
from jax.sharding import PartitionSpec as P

AXES = ("row", "col")
LANES = 128
BF16 = jnp.bfloat16
F32 = jnp.float32
NN = (((1,), (0,)), ((), ()))
NT = (((1,), (1,)), ((), ()))
TN = (((0,), (0,)), ((), ()))


def split_table(table):
    high = table.astype(np.float32).astype(jnp.bfloat16)
    low = (table - high.astype(np.float64)).astype(np.float32).astype(jnp.bfloat16)
    return high, low


def wave_tables(extent):
    freqs = np.arange(extent)[:, None] + 0.5
    cells = np.arange(extent)[None, :]
    angles = np.pi / extent * freqs * (cells - (extent - 1) / 2)
    waves = np.concatenate([np.cos(angles), np.sin(angles)], axis=0)
    weights = np.where(cells == 0, 1.0, 2.0)
    even = weights * np.cos(np.pi / extent * freqs * cells)
    return waves, even


def split(value):
    high = value.astype(BF16)
    low = (value - high.astype(F32)).astype(BF16)
    return high, low


def dot3(left, right, dims):
    lh, ll = left
    rh, rl = right

    def dot(a, b):
        return lax.dot_general(a, b, dims, preferred_element_type=F32)

    return dot(lh, rh) + (dot(lh, rl) + dot(ll, rh))


def whole(shape):
    return pl.BlockSpec(shape, lambda *_: (0,) * len(shape))


def z_forward(lines, tables, pairs):
    rows, extent = lines.shape
    n_out = tables[0].shape[0] // extent

    def body(x_ref, th_ref, tl_ref, *out_refs):
        step = pl.program_id(0)
        right = split(x_ref[...])
        for o, out_ref in enumerate(out_refs):
            part = slice(o * extent, (o + 1) * extent)
            acc = dot3((th_ref[part, :], tl_ref[part, :]), right, NT)
            for h in range(2):
                out_ref[pl.ds(2 * step + h, extent, stride=pairs), :] = acc[:, h * LANES : (h + 1) * LANES]

    return pl.pallas_call(
        body,
        grid=(pairs // 2,),
        in_specs=[pl.BlockSpec((2 * LANES, extent), lambda i: (i, 0)), whole(tables[0].shape), whole(tables[1].shape)],
        out_specs=[whole((extent * pairs, LANES))] * n_out,
        out_shape=[jax.ShapeDtypeStruct((extent * pairs, LANES), F32)] * n_out,
        cost_estimate=pl.CostEstimate(flops=6 * rows * extent * extent * n_out, transcendentals=0, bytes_accessed=4 * rows * extent * (1 + n_out)),
        name="z_forward",
    )(lines, *tables)


def z_inverse(received, tables, pairs, extent, partial):
    rows = pairs * LANES

    def body(r_ref, th_ref, tl_ref, *rest):
        out_ref = rest[-1]
        step = pl.program_id(0)
        left = jnp.concatenate(
            [r_ref[pl.ds(2 * step + h, extent, stride=pairs), :] for h in range(2)], axis=1
        )
        acc = dot3(split(left), (th_ref[...], tl_ref[...]), TN)
        if partial is not None:
            acc = acc + rest[0][...]
        out_ref[...] = acc

    lines = pl.BlockSpec((2 * LANES, extent), lambda i: (i, 0))
    extra = [] if partial is None else [partial]
    return pl.pallas_call(
        body,
        grid=(pairs // 2,),
        in_specs=[whole(received.shape), whole(tables[0].shape), whole(tables[1].shape)] + [lines] * len(extra),
        out_specs=lines,
        out_shape=jax.ShapeDtypeStruct((rows, extent), F32),
        cost_estimate=pl.CostEstimate(flops=6 * rows * extent * extent, transcendentals=0, bytes_accessed=8 * rows * extent),
        name="z_inverse",
    )(received, *tables, *extra)


def lane_half(shape):
    return lax.broadcasted_iota(jnp.int32, shape, 1) < LANES // 2


def swap(value):
    return pltpu.roll(value, LANES // 2, 1)


def read_plane(ref, plane_ref):
    n_row, n_col, _, pairs, _ = ref.shape
    half_x = n_row * pairs
    mask = lane_half((half_x, LANES))
    for p in range(n_col // 2):
        a = ref[:, 2 * p, 0].reshape(half_x, LANES)
        b = ref[:, 2 * p + 1, 0].reshape(half_x, LANES)
        lanes = slice(p * LANES, (p + 1) * LANES)
        plane_ref[:half_x, lanes] = jnp.where(mask, a, swap(b))
        plane_ref[half_x:, lanes] = jnp.where(mask, swap(a), b)


def write_plane(ref, plane):
    n_row, n_col, _, pairs, _ = ref.shape
    half_x = n_row * pairs
    mask = lane_half((half_x, LANES))
    for p in range(n_col // 2):
        lanes = slice(p * LANES, (p + 1) * LANES)
        q0 = plane[:half_x, lanes]
        q1 = plane[half_x:, lanes]
        ref[:, 2 * p, 0] = jnp.where(mask, q0, swap(q1)).reshape(n_row, pairs, LANES)
        ref[:, 2 * p + 1, 0] = jnp.where(mask, swap(q0), q1).reshape(n_row, pairs, LANES)


def block_of(shape):
    n_row, n_col, _, pairs, lanes = shape
    return pl.BlockSpec((n_row, n_col, 1, pairs, lanes), lambda k: (0, 0, k, 0, 0))


def kernel_planes(received, x_tables, y_tables, extent):
    planes = received.shape[2]
    scaling = 1.0 / float(extent) ** 3

    def body(r_ref, xh, xl, yh, yl, out_ref, plane_ref):
        read_plane(r_ref, plane_ref)
        first = dot3((xh[...], xl[...]), split(plane_ref[...]), NN)
        out_ref[0] = dot3(split(first), (yh[...], yl[...]), NT) * scaling

    tables = (*x_tables, *y_tables)
    return pl.pallas_call(
        body,
        grid=(planes,),
        in_specs=[block_of(received.shape)] + [whole(t.shape) for t in tables],
        out_specs=pl.BlockSpec((1, extent, extent), lambda k: (k, 0, 0)),
        out_shape=jax.ShapeDtypeStruct((planes, extent, extent), F32),
        scratch_shapes=[pltpu.VMEM((extent, extent), F32)],
        cost_estimate=pl.CostEstimate(flops=12 * planes * extent**3, transcendentals=0, bytes_accessed=8 * planes * extent**2),
        name="kernel_planes",
    )(received, *tables)


def convolve_planes(received, kernel, x_tables, y_tables, extent):
    planes = received.shape[2]
    block = LANES

    def body(r_ref, k_ref, xh, xl, yh, yl, out_ref, plane_ref, wh_ref, wl_ref):
        read_plane(r_ref, plane_ref)
        plane = split(plane_ref[...])
        y_table = (yh[...], yl[...])
        for i in range(2 * extent // block):
            rows = slice(i * block, (i + 1) * block)
            start = i * block % extent
            along_x = dot3((xh[rows, :], xl[rows, :]), plane, NN)
            spectrum = dot3(split(along_x), y_table, NT)
            weight = k_ref[0, start : start + block, :]
            spectrum = spectrum * jnp.concatenate([weight, weight], axis=1)
            high, low = split(dot3(split(spectrum), y_table, NN))
            wh_ref[rows, :] = high
            wl_ref[rows, :] = low
        result = dot3((xh[...], xl[...]), (wh_ref[...], wl_ref[...]), TN)
        write_plane(out_ref, result)

    tables = (*x_tables, *y_tables)
    return pl.pallas_call(
        body,
        grid=(planes,),
        in_specs=[block_of(received.shape), pl.BlockSpec((1, extent, extent), lambda k: (k, 0, 0))]
        + [whole(t.shape) for t in tables],
        out_specs=block_of(received.shape),
        out_shape=jax.ShapeDtypeStruct(received.shape, F32),
        scratch_shapes=[
            pltpu.VMEM((extent, extent), F32),
            pltpu.VMEM((2 * extent, extent), BF16),
            pltpu.VMEM((2 * extent, extent), BF16),
        ],
        cost_estimate=pl.CostEstimate(flops=72 * planes * extent**3, transcendentals=0, bytes_accessed=12 * planes * extent**2),
        name="convolve_planes",
    )(received, kernel, *tables)


def solution(mesh):
    n_row, n_col = mesh.shape["row"], mesh.shape["col"]
    n_dev = n_row * n_col

    def on_device(density, green_octant):
        local_x, local_y, extent = density.shape
        pairs = local_x * local_y // LANES
        planes = extent // n_dev
        waves, even = wave_tables(extent)
        order = np.arange(extent).reshape(n_row, pairs, 2).transpose(2, 0, 1).reshape(-1)
        y_waves = split_table(waves)
        x_waves = split_table(waves[:, order])
        y_even = split_table(even)
        x_even = split_table(even[:, order])

        def exchange(value):
            value = value.reshape(n_dev, planes * pairs, LANES)
            return lax.all_to_all(value, AXES, 0, 0)

        def by_plane(value):
            return value.reshape(n_row, n_col, planes, pairs, LANES)

        (green_z,) = z_forward(green_octant.reshape(-1, extent), y_even, pairs)
        green_k = exchange(green_z)
        cos_z, sin_z = z_forward(density.reshape(-1, extent), y_waves, pairs)
        cos_k = exchange(cos_z)
        sin_k = exchange(sin_z)
        kernel = kernel_planes(by_plane(green_k), x_even, y_even, extent)
        cos_p = convolve_planes(by_plane(cos_k), kernel, x_waves, y_waves, extent)
        cos_b = exchange(cos_p)
        sin_p = convolve_planes(by_plane(sin_k), kernel, x_waves, y_waves, extent)
        sin_b = exchange(sin_p)
        cos_t = tuple(t[:extent] for t in y_waves)
        sin_t = tuple(t[extent:] for t in y_waves)
        partial = z_inverse(cos_b.reshape(-1, LANES), cos_t, pairs, extent, None)
        result = z_inverse(sin_b.reshape(-1, LANES), sin_t, pairs, extent, partial)
        return result.reshape(local_x, local_y, extent)

    return jax.shard_map(
        on_device,
        mesh=mesh,
        in_specs=(P("row", "col", None), P("row", "col", None)),
        out_specs=P("row", "col", None),
        check_vma=False,
    )
```

time: 1020 us -> 282 us (0.28); the launches traced: 1010 us -> 281 us
  local copies, waits for them, and re-layouts: 386 us -> 3.97 us
  matrix products: 246 us -> 0 us
  other arithmetic: 162 us -> 0 us
  Pallas kernels: 0 us -> 103 us
  starting transfers between devices: 80.1 us -> 16.5 us
  blocking collectives: 21.2 us -> 52.1 us
    unnamed x18 -> x0, matrix products: 187 us -> none
    all_to_all x31 -> x0, local copies, waits for them, and re-layouts: 162 us -> none  [the longest x2 20.7 us: on_device(): lax.all_to_all(imaginary, 'col', split_axis=2, concat_axis=1, tiled=True)]
    unnamed x64 -> x8, local copies, waits for them, and re-layouts: 150 us -> 3.97 us
    all_to_all x15 -> x0, other arithmetic: 116 us -> none  [the longest x1 14.1 us: on_device(): lax.all_to_all(imaginary, 'row', split_axis=1, concat_axis=0, tiled=True)]
    pallas_call x0 -> x7, Pallas kernels: none -> 103 us  [the longest x2 64.3 us: convolve_planes(): pl.pallas_call(body, grid=(planes,), in_specs=[block_of(received.shape),...]
    all_to_all x15 -> x4, starting transfers between devices: 80.1 us -> 16.5 us  [exchange(): return lax.all_to_all(value, AXES, 0, 0)]
    dot_general x21 -> x0, matrix products: 58.9 us -> none  [contract(): jnp.einsum(pattern, operand, matrix, precision=lax.Precision.HIGHEST, pre...]
    all_to_all x0 -> x1, blocking collectives: none -> 52.1 us  [exchange(): return lax.all_to_all(value, AXES, 0, 0)]
  transfers between devices with their start and end apart: 15 -> 4, of which waited for: 5 -> 4; matrix products, arithmetic and copies ran while one was open for 70% -> 0% of each run, Pallas kernels for 0% -> 31%
where the time goes in v1:
time: 282 us; the launch traced here: 281 us
  waiting for transfers between devices  105 us (37%)
  Pallas kernels  103 us (37%)
  blocking collectives  52.1 us (18%)
  starting transfers between devices  16.5 us (6%)
  local copies, waits for them, and re-layouts  3.97 us (1%)
    all_to_all x4, waiting for transfers between devices, exchange(): return lax.all_to_all(value, AXES, 0, 0)  105 us
    pallas_call x2, Pallas kernels, convolve_planes(): pl.pallas_call(body, grid=(planes,), in_specs=[block_of(received.shape),...  64.3 us
    all_to_all x1, blocking collectives, exchange(): return lax.all_to_all(value, AXES, 0, 0)  52.1 us
    all_to_all x4, starting transfers between devices, exchange(): return lax.all_to_all(value, AXES, 0, 0)  16.5 us
    pallas_call x2, Pallas kernels, z_forward(): pl.pallas_call(body, grid=(pairs // 2,), in_specs=[pl.BlockSpec((2 * LANE...  15.9 us
    pallas_call x2, Pallas kernels, z_inverse(): pl.pallas_call(body, grid=(pairs // 2,), in_specs=[whole(received.shape),...  14.5 us
    pallas_call x1, Pallas kernels, kernel_planes(): pl.pallas_call(body, grid=(planes,), in_specs=[block_of(received.shape)]...  8.7 us
  transfers between devices with their start and end apart: 4, of which 4 were waited for; matrix products, arithmetic and copies ran while one was open for 0% of the time, Pallas kernels for 31%

profile of v1, /device:TPU:1, one launch (start us, length us, event | category | flops | bytes accessed | tf_op | source)
XLA Modules:
  0.0 280.9 jit_solution(12629890820810511531)
XLA Ops:
  0.0 7.1 %z_forward.3 = f32[4096,128]{1,0:T(8,128)} custom-call(f32[2048,256]{1,0:T(8,128)} %bitcast.16, bf16[256,256]{1,0:T(8,128)(2,1)} %constant.24.clone.th_ref.yh, bf16[256,256]{1,0:T(8,128)(2,1)} %constant.25.clone.tl_ref.yl), custom_call_target="tpu_custom_call" | custom-call | flops 805306368 | bytes 4194304 | tf_op jit(solution)/shard_map/z_forward/pallas_call | solution.py:67
  7.1 7.1 %all-to-all-start.1 = ((f32[32,128,128]{2,1,0:T(8,128)}), f32[32,128,128]{2,1,0:T(8,128)S(1)}, u32[]{:S(2)}, u32[]{:S(2)}) async-start(f32[32,128,128]{2,1,0:T(8,128)} %bitcast.15), calls=%async_computation.1 | async-start | bytes 4194304 | tf_op jit(solution)/shard_map/all_to_all | solution.py:220
  14.2 8.8 %z_forward.2 = (f32[4096,128]{1,0:T(8,128)}, f32[4096,128]{1,0:T(8,128)}) custom-call(f32[2048,256]{1,0:T(8,128)} %bitcast.24, bf16[512,256]{1,0:T(8,128)(2,1)} %constant.26.clone.th_ref.yh, bf16[512,256]{1,0:T(8,128)(2,1)} %constant.27.clone.tl_ref.yl), custom_call_target="tpu_custom_call" | custom-call | flops 1610612736 | bytes 6291456 | tf_op jit(solution)/shard_map/z_forward/pallas_call | solution.py:67
  23.0 39.5 %all-to-all-done.1 = f32[32,128,128]{2,1,0:T(8,128)S(1)} async-done(((f32[32,128,128]{2,1,0:T(8,128)}), f32[32,128,128]{2,1,0:T(8,128)S(1)}, u32[]{:S(2)}, u32[]{:S(2)}) %all-to-all-start.1) | async-done | bytes 2097184 | tf_op jit(solution)/shard_map/all_to_all | solution.py:220
  62.5 0.0 copy-start.3
  62.5 52.1 %all_to_all.25 = f32[32,128,128]{2,1,0:T(8,128)} all-to-all(f32[32,128,128]{2,1,0:T(8,128)} %bitcast.23), channel_id=1, replica_groups=mesh['row'=8,'col'=4] {'row','col'}, dimensions={0} | all-to-all | bytes 4194304 | tf_op jit(solution)/shard_map/all_to_all | solution.py:220
  114.6 0.0 copy-done.3
  114.6 3.2 %all-to-all-start = ((f32[32,128,128]{2,1,0:T(8,128)}), f32[32,128,128]{2,1,0:T(8,128)S(1)}, u32[]{:S(2)}, u32[]{:S(2)}) async-start(f32[32,128,128]{2,1,0:T(8,128)} %bitcast.19), calls=%async_computation | async-start | bytes 4194304 | tf_op jit(solution)/shard_map/all_to_all | solution.py:220
  117.7 8.7 %kernel_planes.1.k_ref = f32[8,256,256]{2,1,0:T(8,128)} custom-call(f32[8,4,8,16,128]{4,3,2,1,0:T(8,128)} %bitcast.18, bf16[256,256]{1,0:T(8,128)(2,1)} %constant.28.clone.xh, bf16[256,256]{1,0:T(8,128)(2,1)} %constant.29.clone.xl, bf16[256,256]{1,0:T(8,128)(2,1)} %constant.24.clone.th_ref.yh, bf16[256,256]{1,0:T(8,128)(2,1)} %constant.25.clone.tl_ref.yl), custom_call_target="tpu_custom_call" | custom-call | flops 1610612736 | bytes 4194304 | tf_op jit(solution)/shard_map/kernel_planes/pallas_call | solution.py:152
  126.4 32.1 %convolve_planes.3 = f32[8,4,8,16,128]{4,3,2,1,0:T(8,128)} custom-call(f32[8,4,8,16,128]{4,3,2,1,0:T(8,128)} %bitcast.22, f32[8,256,256]{2,1,0:T(8,128)} %kernel_planes.1.k_ref, bf16[512,256]{1,0:T(8,128)(2,1)} %constant.30.clone.xh, bf16[512,256]{1,0:T(8,128)(2,1)} %constant.31.clone.xl, bf16[512,256]{1,0:T(8,128)(2,1)} %constant.26.clone.th_ref.yh, ...), custom_call_target="tpu_custom_call" | custom-call | flops 9663676416 | bytes 6291456 | tf_op jit(solution)/shard_map/convolve_planes/pallas_call | solution.py:186
  158.6 7.5 %all-to-all-done = f32[32,128,128]{2,1,0:T(8,128)S(1)} async-done(((f32[32,128,128]{2,1,0:T(8,128)}), f32[32,128,128]{2,1,0:T(8,128)S(1)}, u32[]{:S(2)}, u32[]{:S(2)}) %all-to-all-start) | async-done | bytes 2097184 | tf_op jit(solution)/shard_map/all_to_all | solution.py:220
  166.1 0.0 copy-start.2
  166.1 1.3 copy-done.2
  167.4 3.2 %all-to-all-start.4 = ((f32[32,128,128]{2,1,0:T(8,128)}), f32[32,128,128]{2,1,0:T(8,128)S(1)}, u32[]{:S(2)}, u32[]{:S(2)}) async-start(f32[32,128,128]{2,1,0:T(8,128)} %bitcast.21), calls=%async_computation.4 | async-start | bytes 4194304 | tf_op jit(solution)/shard_map/all_to_all | solution.py:220
  170.5 32.1 %convolve_planes.2 = f32[8,4,8,16,128]{4,3,2,1,0:T(8,128)} custom-call(f32[8,4,8,16,128]{4,3,2,1,0:T(8,128)} %bitcast.17, f32[8,256,256]{2,1,0:T(8,128)} %kernel_planes.1.k_ref, bf16[512,256]{1,0:T(8,128)(2,1)} %constant.30.clone.xh, bf16[512,256]{1,0:T(8,128)(2,1)} %constant.31.clone.xl, bf16[512,256]{1,0:T(8,128)(2,1)} %constant.26.clone.th_ref.yh, ...), custom_call_target="tpu_custom_call" | custom-call | flops 9663676416 | bytes 6291456 | tf_op jit(solution)/shard_map/convolve_planes/pallas_call | solution.py:186
  202.7 16.2 %all-to-all-done.4 = f32[32,128,128]{2,1,0:T(8,128)S(1)} async-done(((f32[32,128,128]{2,1,0:T(8,128)}), f32[32,128,128]{2,1,0:T(8,128)S(1)}, u32[]{:S(2)}, u32[]{:S(2)}) %all-to-all-start.4) | async-done | bytes 2097184 | tf_op jit(solution)/shard_map/all_to_all | solution.py:220
  218.9 0.0 copy-start.1
  218.9 1.3 copy-done.1
  220.2 3.2 %all-to-all-start.2 = ((f32[32,128,128]{2,1,0:T(8,128)}), f32[32,128,128]{2,1,0:T(8,128)S(1)}, u32[]{:S(2)}, u32[]{:S(2)}) async-start(f32[32,128,128]{2,1,0:T(8,128)} %bitcast.20), calls=%async_computation.2 | async-start | bytes 4194304 | tf_op jit(solution)/shard_map/all_to_all | solution.py:220
  223.3 6.6 %z_inverse.2.rest_0_ = f32[2048,256]{1,0:T(8,128)} custom-call(f32[4096,128]{1,0:T(8,128)} %bitcast.14, bf16[256,256]{1,0:T(8,128)(2,1)} %constant.32.clone.th_ref, bf16[256,256]{1,0:T(8,128)(2,1)} %constant.33.clone.tl_ref), custom_call_target="tpu_custom_call" | custom-call | flops 805306368 | bytes 4194304 | tf_op jit(solution)/shard_map/z_inverse/pallas_call | solution.py:94
  229.9 41.8 %all-to-all-done.2 = f32[32,128,128]{2,1,0:T(8,128)S(1)} async-done(((f32[32,128,128]{2,1,0:T(8,128)}), f32[32,128,128]{2,1,0:T(8,128)S(1)}, u32[]{:S(2)}, u32[]{:S(2)}) %all-to-all-start.2) | async-done | bytes 2097184 | tf_op jit(solution)/shard_map/all_to_all | solution.py:220
  271.6 0.0 copy-start
  271.6 1.3 copy-done
  273.0 7.9 %z_inverse.3 = f32[2048,256]{1,0:T(8,128)} custom-call(f32[4096,128]{1,0:T(8,128)} %bitcast.13, bf16[256,256]{1,0:T(8,128)(2,1)} %constant.34.clone.th_ref, bf16[256,256]{1,0:T(8,128)(2,1)} %constant.35.clone.tl_ref, f32[2048,256]{1,0:T(8,128)} %z_inverse.2.rest_0_), custom_call_target="tpu_custom_call" | custom-call | flops 805306368 | bytes 4194304 | tf_op jit(solution)/shard_map/z_inverse/pallas_call | solution.py:94
Async XLA Ops:
  7.1 55.4 %all-to-all-start.1 = ((f32[32,128,128]{2,1,0:T(8,128)}), f32[32,128,128]{2,1,0:T(8,128)S(1)}, u32[]{:S(2)}, u32[]{:S(2)}) async-start(f32[32,128,128]{2,1,0:T(8,128)} %bitcast.15), calls=%async_computation.1 | async-start | bytes 4194304 | tf_op jit(solution)/shard_map/all_to_all | solution.py:220
  62.5 52.1 %copy-start.3 = (f32[32,128,128]{2,1,0:T(8,128)}, f32[32,128,128]{2,1,0:T(8,128)S(1)}, u32[]{:S(2)}) copy-start(f32[32,128,128]{2,1,0:T(8,128)S(1)} %all-to-all-done.1) | copy-start | bytes 6291460
  114.6 51.5 %all-to-all-start = ((f32[32,128,128]{2,1,0:T(8,128)}), f32[32,128,128]{2,1,0:T(8,128)S(1)}, u32[]{:S(2)}, u32[]{:S(2)}) async-start(f32[32,128,128]{2,1,0:T(8,128)} %bitcast.19), calls=%async_computation | async-start | bytes 4194304 | tf_op jit(solution)/shard_map/all_to_all | solution.py:220
  166.1 1.3 copy-start.2
  167.4 51.5 %all-to-all-start.4 = ((f32[32,128,128]{2,1,0:T(8,128)}), f32[32,128,128]{2,1,0:T(8,128)S(1)}, u32[]{:S(2)}, u32[]{:S(2)}) async-start(f32[32,128,128]{2,1,0:T(8,128)} %bitcast.21), calls=%async_computation.4 | async-start | bytes 4194304 | tf_op jit(solution)/shard_map/all_to_all | solution.py:220
  218.9 1.3 copy-start.1
  220.2 51.5 %all-to-all-start.2 = ((f32[32,128,128]{2,1,0:T(8,128)}), f32[32,128,128]{2,1,0:T(8,128)S(1)}, u32[]{:S(2)}, u32[]{:S(2)}) async-start(f32[32,128,128]{2,1,0:T(8,128)} %bitcast.20), calls=%async_computation.2 | async-start | bytes 4194304 | tf_op jit(solution)/shard_map/all_to_all | solution.py:220
  271.6 1.3 copy-start

commit v2 on v1

v2 whole, which is shorter than its diff:
```python
import numpy as np
import jax
import jax.numpy as jnp
from jax import lax
from jax.experimental import pallas as pl
from jax.experimental.pallas import tpu as pltpu
from jax.sharding import PartitionSpec as P

AXES = ("row", "col")
LANES = 128
BF16 = jnp.bfloat16
F32 = jnp.float32
NN = (((1,), (0,)), ((), ()))
NT = (((1,), (1,)), ((), ()))
TN = (((0,), (0,)), ((), ()))


def split_table(table):
    high = table.astype(np.float32).astype(jnp.bfloat16)
    low = (table - high.astype(np.float64)).astype(np.float32).astype(jnp.bfloat16)
    return high, low


def wave_tables(extent):
    freqs = np.arange(extent)[:, None] + 0.5
    cells = np.arange(extent)[None, :]
    angles = np.pi / extent * freqs * (cells - (extent - 1) / 2)
    waves = np.concatenate([np.cos(angles), np.sin(angles)], axis=0)
    weights = np.where(cells == 0, 1.0, 2.0)
    even = weights * np.cos(np.pi / extent * freqs * cells)
    return waves, even


def split(value):
    high = value.astype(BF16)
    low = (value - high.astype(F32)).astype(BF16)
    return high, low


def stack_left(high, low, axis):
    return jnp.concatenate([high, high, low], axis=axis)


def stack_right(high, low, axis):
    return jnp.concatenate([high, low, high], axis=axis)


def dot(left, right, dims):
    return lax.dot_general(left, right, dims, preferred_element_type=F32)


def whole(shape):
    return pl.BlockSpec(shape, lambda *_: (0,) * len(shape))


def z_forward(sources, n_dev, pairs):
    rows, extent = sources[0][0].shape
    planes = extent // n_dev
    width = planes * len(sources)
    per = min(8, pairs)
    n = len(sources)

    def body(*refs):
        out_ref = refs[-1]
        step = pl.program_id(0)
        for g in range(n):
            x_ref, h_ref, l_ref = refs[3 * g : 3 * g + 3]
            right = stack_right(*split(x_ref[...]), 1)
            acc = dot(stack_left(h_ref[...], l_ref[...], 1), right, NT)
            for h in range(per):
                for d in range(n_dev):
                    start = (d * width + g * planes) * pairs + per * step + h
                    out_ref[pl.ds(start, planes, stride=pairs), :] = acc[
                        d * planes : (d + 1) * planes, h * LANES : (h + 1) * LANES
                    ]

    lines = pl.BlockSpec((per * LANES, extent), lambda i: (i, 0))
    table = whole((extent, extent))
    return pl.pallas_call(
        body,
        grid=(pairs // per,),
        in_specs=[lines, table, table] * n,
        out_specs=whole((n_dev * width * pairs, LANES)),
        out_shape=jax.ShapeDtypeStruct((n_dev * width * pairs, LANES), F32),
        cost_estimate=pl.CostEstimate(flops=6 * rows * extent * extent * n, transcendentals=0, bytes_accessed=8 * rows * extent * n),
        name="z_forward",
    )(*[a for source in sources for a in source])


def z_inverse(received, tables, pairs, extent, partial):
    rows = pairs * LANES
    per = min(8, pairs)

    def body(r_ref, h_ref, l_ref, *rest):
        out_ref = rest[-1]
        step = pl.program_id(0)
        left = jnp.concatenate(
            [r_ref[pl.ds(per * step + h, extent, stride=pairs), :] for h in range(per)], axis=1
        )
        acc = dot(stack_right(*split(left), 0), stack_left(h_ref[...], l_ref[...], 0), TN)
        if partial is not None:
            acc = acc + rest[0][...]
        out_ref[...] = acc

    lines = pl.BlockSpec((per * LANES, extent), lambda i: (i, 0))
    extra = [] if partial is None else [partial]
    table = whole((extent, extent))
    return pl.pallas_call(
        body,
        grid=(pairs // per,),
        in_specs=[pl.BlockSpec(memory_space=pltpu.VMEM), table, table] + [lines] * len(extra),
        out_specs=lines,
        out_shape=jax.ShapeDtypeStruct((rows, extent), F32),
        cost_estimate=pl.CostEstimate(flops=6 * rows * extent * extent, transcendentals=0, bytes_accessed=8 * rows * extent),
        name="z_inverse",
    )(received, *tables, *extra)


def lane_half(shape):
    return lax.broadcasted_iota(jnp.int32, shape, 1) < LANES // 2


def swap(value):
    return pltpu.roll(value, LANES // 2, 1)


def read_plane(ref, index, plane_ref):
    n_row, n_col, _, pairs, _ = ref.shape
    half_x = n_row * pairs
    mask = lane_half((half_x, LANES))
    for p in range(n_col // 2):
        a = ref[:, 2 * p, index].reshape(half_x, LANES)
        b = ref[:, 2 * p + 1, index].reshape(half_x, LANES)
        lanes = slice(p * LANES, (p + 1) * LANES)
        plane_ref[:half_x, lanes] = jnp.where(mask, a, swap(b))
        plane_ref[half_x:, lanes] = jnp.where(mask, swap(a), b)


def write_plane(ref, plane):
    n_row, n_col, _, pairs, _ = ref.shape
    half_x = n_row * pairs
    mask = lane_half((half_x, LANES))
    for p in range(n_col // 2):
        lanes = slice(p * LANES, (p + 1) * LANES)
        q0 = plane[:half_x, lanes]
        q1 = plane[half_x:, lanes]
        ref[:, 2 * p, 0] = jnp.where(mask, q0, swap(q1)).reshape(n_row, pairs, LANES)
        ref[:, 2 * p + 1, 0] = jnp.where(mask, swap(q0), q1).reshape(n_row, pairs, LANES)


def kernel_planes(received, offset, planes, x_tables, y_tables, extent):
    scaling = 1.0 / float(extent) ** 3

    def body(r_ref, xh, xl, yh, yl, out_ref, plane_ref):
        read_plane(r_ref, offset + pl.program_id(0), plane_ref)
        first = dot(stack_left(xh[...], xl[...], 1), stack_right(*split(plane_ref[...]), 0), NN)
        second = dot(stack_left(*split(first), 1), stack_right(yh[...], yl[...], 1), NT)
        out_ref[0] = second * scaling

    tables = (*x_tables, *y_tables)
    return pl.pallas_call(
        body,
        grid=(planes,),
        in_specs=[pl.BlockSpec(memory_space=pltpu.VMEM)] + [whole(t.shape) for t in tables],
        out_specs=pl.BlockSpec((1, extent, extent), lambda k: (k, 0, 0)),
        out_shape=jax.ShapeDtypeStruct((planes, extent, extent), F32),
        scratch_shapes=[pltpu.VMEM((extent, extent), F32)],
        cost_estimate=pl.CostEstimate(flops=12 * planes * extent**3, transcendentals=0, bytes_accessed=8 * planes * extent**2),
        name="kernel_planes",
    )(received, *tables)


def convolve_planes(received, offset, kernel, x_tables, xt_tables, y_tables, extent):
    planes = kernel.shape[0]
    n_row, n_col, _, pairs, _ = received.shape

    def body(r_ref, k_ref, xh, xl, th, tl, yh, yl, out_ref, plane_ref):
        read_plane(r_ref, offset + pl.program_id(0), plane_ref)
        along_x = dot(stack_left(xh[...], xl[...], 1), stack_right(*split(plane_ref[...]), 0), NN)
        spectrum = dot(stack_left(*split(along_x), 1), stack_right(yh[...], yl[...], 1), NT)
        weight = k_ref[0]
        weight = jnp.concatenate([weight, weight], axis=1)
        spectrum = spectrum * jnp.concatenate([weight, weight], axis=0)
        along_y = dot(stack_left(*split(spectrum), 1), stack_right(yh[...], yl[...], 0), NN)
        result = dot(stack_left(th[...], tl[...], 1), stack_right(*split(along_y), 0), NN)
        write_plane(out_ref, result)

    tables = (*x_tables, *xt_tables, *y_tables)
    shape = (n_row, n_col, planes, pairs, LANES)
    return pl.pallas_call(
        body,
        grid=(planes,),
        in_specs=[pl.BlockSpec(memory_space=pltpu.VMEM), pl.BlockSpec((1, extent, extent), lambda k: (k, 0, 0))]
        + [whole(t.shape) for t in tables],
        out_specs=pl.BlockSpec((n_row, n_col, 1, pairs, LANES), lambda k: (0, 0, k, 0, 0)),
        out_shape=jax.ShapeDtypeStruct(shape, F32),
        scratch_shapes=[pltpu.VMEM((extent, extent), F32)],
        cost_estimate=pl.CostEstimate(flops=72 * planes * extent**3, transcendentals=0, bytes_accessed=12 * planes * extent**2),
        name="convolve_planes",
    )(received, kernel, *tables)


def solution(mesh):
    n_row, n_col = mesh.shape["row"], mesh.shape["col"]
    n_dev = n_row * n_col

    def on_device(density, green_octant):
        local_x, local_y, extent = density.shape
        pairs = local_x * local_y // LANES
        planes = extent // n_dev
        waves, even = wave_tables(extent)
        order = np.arange(extent).reshape(n_row, pairs, 2).transpose(2, 0, 1).reshape(-1)
        y_waves = split_table(waves)
        x_waves = split_table(waves[:, order])
        xt_waves = split_table(waves[:, order].T)
        y_even = split_table(even)
        x_even = split_table(even[:, order])
        cos_z = split_table(waves[:extent])
        sin_z = split_table(waves[extent:])

        def exchange(value):
            value = lax.all_to_all(value.reshape(n_dev, -1, LANES), AXES, 0, 0)
            return value.reshape(n_row, n_col, -1, pairs, LANES)

        dens = density.reshape(-1, extent)
        green = green_octant.reshape(-1, extent)
        first = exchange(z_forward([(green, *y_even), (dens, *cos_z)], n_dev, pairs))
        second = exchange(z_forward([(dens, *sin_z)], n_dev, pairs))
        kernel = kernel_planes(first, 0, planes, x_even, y_even, extent)
        cos_p = convolve_planes(first, planes, kernel, x_waves, xt_waves, y_waves, extent)
        cos_b = exchange(cos_p)
        sin_p = convolve_planes(second, 0, kernel, x_waves, xt_waves, y_waves, extent)
        sin_b = exchange(sin_p)
        partial = z_inverse(cos_b.reshape(-1, LANES), cos_z, pairs, extent, None)
        result = z_inverse(sin_b.reshape(-1, LANES), sin_z, pairs, extent, partial)
        return result.reshape(local_x, local_y, extent)

    return jax.shard_map(
        on_device,
        mesh=mesh,
        in_specs=(P("row", "col", None), P("row", "col", None)),
        out_specs=P("row", "col", None),
        check_vma=False,
    )
```

time: 282 us -> 272 us (0.965)
  waiting for transfers between devices: 105 us -> 174 us
  blocking collectives: 52.1 us -> 0 us
  Pallas kernels: 103 us -> 73.8 us
    all_to_all x4, waiting for transfers between devices: 105 us -> 174 us  [exchange(): value = lax.all_to_all(value.reshape(n_dev, -1, LANES), AXES, 0, 0)]
    all_to_all x1 -> x0, blocking collectives: 52.1 us -> none  [exchange(): return lax.all_to_all(value, AXES, 0, 0)]
    pallas_call x7, Pallas kernels: 103 us -> 73.8 us  [the longest x2 45 us: convolve_planes(): pl.pallas_call(body, grid=(planes,), in_specs=[pl.BlockSpec(memory_space=...]
  transfers between devices with their start and end apart: 4 -> 4, of which waited for: 4 -> 4; matrix products, arithmetic and copies ran while one was open for 0% -> 0% of each run, Pallas kernels for 31% -> 23%
where the time goes in v2:
time: 272 us; the launch traced here: 271 us
  waiting for transfers between devices  174 us (64%)
  Pallas kernels  73.8 us (27%)
  starting transfers between devices  19.3 us (7%)
  local copies, waits for them, and re-layouts  3.97 us (1%)
    all_to_all x4, waiting for transfers between devices, exchange(): value = lax.all_to_all(value.reshape(n_dev, -1, LANES), AXES, 0, 0)  174 us
    pallas_call x2, Pallas kernels, convolve_planes(): pl.pallas_call(body, grid=(planes,), in_specs=[pl.BlockSpec(memory_space=...  45 us
    all_to_all x4, starting transfers between devices, exchange(): value = lax.all_to_all(value.reshape(n_dev, -1, LANES), AXES, 0, 0)  19.3 us
    pallas_call x2, Pallas kernels, z_forward(): pl.pallas_call(body, grid=(pairs // per,), in_specs=[lines, table, table]...  10.6 us
    pallas_call x2, Pallas kernels, z_inverse(): pl.pallas_call(body, grid=(pairs // per,), in_specs=[pl.BlockSpec(memory_...  9.43 us
    pallas_call x1, Pallas kernels, kernel_planes(): pl.pallas_call(body, grid=(planes,), in_specs=[pl.BlockSpec(memory_space=...  8.83 us
  transfers between devices with their start and end apart: 4, of which 4 were waited for; matrix products, arithmetic and copies ran while one was open for 0% of the time, Pallas kernels for 23%

profile of v2, /device:TPU:1, one launch (start us, length us, event | category | flops | bytes accessed | tf_op | source)
XLA Modules:
  0.0 271.4 jit_solution(14324808448894859554)
XLA Ops:
  0.0 6.4 %z_forward.3 = f32[8192,128]{1,0:T(8,128)} custom-call(f32[2048,256]{1,0:T(8,128)} %bitcast.17, bf16[256,256]{1,0:T(8,128)(2,1)} %constant.28.clone.refs_1_.yh, bf16[256,256]{1,0:T(8,128)(2,1)} %constant.29.clone.refs_2_.yl, f32[2048,256]{1,0:T(8,128)} %bitcast.12, bf16[256,256]{1,0:T(8,128)(2,1)} %constant.30.clone.refs_4_.h_ref, ...), custom_call_target="tpu_custom_call" | custom-call | flops 1610612736 | bytes 8388608 | tf_op jit(solution)/shard_map/z_forward/pallas_call | solution.py:79
  6.4 7.1 %all-to-all-start.1 = ((f32[32,256,128]{2,1,0:T(8,128)}), f32[32,256,128]{2,1,0:T(8,128)}, u32[]{:S(2)}, u32[]{:S(2)}) async-start(f32[32,256,128]{2,1,0:T(8,128)} %bitcast.11), calls=%async_computation.1 | async-start | bytes 8388608 | tf_op jit(solution)/shard_map/all_to_all | solution.py:222
  13.5 4.2 %z_forward.2 = f32[4096,128]{1,0:T(8,128)} custom-call(f32[2048,256]{1,0:T(8,128)} %bitcast.13, bf16[256,256]{1,0:T(8,128)(2,1)} %constant.32.clone.refs_1_.h_ref, bf16[256,256]{1,0:T(8,128)(2,1)} %constant.33.clone.refs_2_.l_ref), custom_call_target="tpu_custom_call" | custom-call | flops 805306368 | bytes 4194304 | tf_op jit(solution)/shard_map/z_forward/pallas_call | solution.py:79
  17.7 87.9 %all-to-all-done.1 = f32[32,256,128]{2,1,0:T(8,128)} async-done(((f32[32,256,128]{2,1,0:T(8,128)}), f32[32,256,128]{2,1,0:T(8,128)}, u32[]{:S(2)}, u32[]{:S(2)}) %all-to-all-start.1) | async-done | bytes 4194336 | tf_op jit(solution)/shard_map/all_to_all | solution.py:222
  105.6 5.8 %all-to-all-start = ((f32[32,128,128]{2,1,0:T(8,128)}), f32[32,128,128]{2,1,0:T(8,128)S(1)}, u32[]{:S(2)}, u32[]{:S(2)}) async-start(f32[32,128,128]{2,1,0:T(8,128)} %bitcast.16), calls=%async_computation | async-start | bytes 4194304 | tf_op jit(solution)/shard_map/all_to_all | solution.py:222
  111.4 8.8 %kernel_planes.1.k_ref = f32[8,256,256]{2,1,0:T(8,128)} custom-call(f32[8,4,16,16,128]{4,3,2,1,0:T(8,128)} %bitcast.5.r_ref, bf16[256,256]{1,0:T(8,128)(2,1)} %constant.34.clone.xh, bf16[256,256]{1,0:T(8,128)(2,1)} %constant.35.clone.xl, bf16[256,256]{1,0:T(8,128)(2,1)} %constant.28.clone.refs_1_.yh, bf16[256,256]{1,0:T(8,128)(2,1)} %constant.29.clone.refs_2_.yl), custom_call_target="tpu_custom_call" | custom-call | flops 1610612736 | bytes 4194304 | tf_op jit(solution)/shard_map/kernel_planes/pallas_call | solution.py:161
  120.2 22.8 %convolve_planes.3 = f32[8,4,8,16,128]{4,3,2,1,0:T(8,128)} custom-call(f32[8,4,16,16,128]{4,3,2,1,0:T(8,128)} %bitcast.5.r_ref, f32[8,256,256]{2,1,0:T(8,128)} %kernel_planes.1.k_ref, bf16[512,256]{1,0:T(8,128)(2,1)} %constant.36.clone.xh, bf16[512,256]{1,0:T(8,128)(2,1)} %constant.37.clone.xl, bf16[256,512]{1,0:T(8,128)(2,1)} %constant.38.clone.th, ...), custom_call_target="tpu_custom_call" | custom-call | flops 9663676416 | bytes 6291456 | tf_op jit(solution)/shard_map/convolve_planes/pallas_call | solution.py:190
  143.0 16.7 %all-to-all-done = f32[32,128,128]{2,1,0:T(8,128)S(1)} async-done(((f32[32,128,128]{2,1,0:T(8,128)}), f32[32,128,128]{2,1,0:T(8,128)S(1)}, u32[]{:S(2)}, u32[]{:S(2)}) %all-to-all-start) | async-done | bytes 2097184 | tf_op jit(solution)/shard_map/all_to_all | solution.py:222
  159.7 0.0 copy-start.2
  159.7 1.3 copy-done.2
  161.0 3.2 %all-to-all-start.3 = ((f32[32,128,128]{2,1,0:T(8,128)}), f32[32,128,128]{2,1,0:T(8,128)S(1)}, u32[]{:S(2)}, u32[]{:S(2)}) async-start(f32[32,128,128]{2,1,0:T(8,128)} %bitcast.20), calls=%async_computation.3 | async-start | bytes 4194304 | tf_op jit(solution)/shard_map/all_to_all | solution.py:222
  164.2 22.2 %convolve_planes.2 = f32[8,4,8,16,128]{4,3,2,1,0:T(8,128)} custom-call(f32[8,4,8,16,128]{4,3,2,1,0:T(8,128)} %bitcast.18, f32[8,256,256]{2,1,0:T(8,128)} %kernel_planes.1.k_ref, bf16[512,256]{1,0:T(8,128)(2,1)} %constant.36.clone.xh, bf16[512,256]{1,0:T(8,128)(2,1)} %constant.37.clone.xl, bf16[256,512]{1,0:T(8,128)(2,1)} %constant.38.clone.th, ...), custom_call_target="tpu_custom_call" | custom-call | flops 9663676416 | bytes 6291456 | tf_op jit(solution)/shard_map/convolve_planes/pallas_call | solution.py:190
  186.4 26.1 %all-to-all-done.3 = f32[32,128,128]{2,1,0:T(8,128)S(1)} async-done(((f32[32,128,128]{2,1,0:T(8,128)}), f32[32,128,128]{2,1,0:T(8,128)S(1)}, u32[]{:S(2)}, u32[]{:S(2)}) %all-to-all-start.3) | async-done | bytes 2097184 | tf_op jit(solution)/shard_map/all_to_all | solution.py:222
  212.5 0.0 copy-start.1
  212.5 1.3 copy-done.1
  213.8 3.2 %all-to-all-start.2 = ((f32[32,128,128]{2,1,0:T(8,128)}), f32[32,128,128]{2,1,0:T(8,128)S(1)}, u32[]{:S(2)}, u32[]{:S(2)}) async-start(f32[32,128,128]{2,1,0:T(8,128)} %bitcast.19), calls=%async_computation.2 | async-start | bytes 4194304 | tf_op jit(solution)/shard_map/all_to_all | solution.py:222
  217.0 4.6 %z_inverse.2.rest_0_ = f32[2048,256]{1,0:T(8,128)} custom-call(f32[4096,128]{1,0:T(8,128)} %bitcast.15, bf16[256,256]{1,0:T(8,128)(2,1)} %constant.30.clone.refs_4_.h_ref, bf16[256,256]{1,0:T(8,128)(2,1)} %constant.31.clone.refs_5_.l_ref), custom_call_target="tpu_custom_call" | custom-call | flops 805306368 | bytes 4194304 | tf_op jit(solution)/shard_map/z_inverse/pallas_call | solution.py:108
  221.6 43.7 %all-to-all-done.2 = f32[32,128,128]{2,1,0:T(8,128)S(1)} async-done(((f32[32,128,128]{2,1,0:T(8,128)}), f32[32,128,128]{2,1,0:T(8,128)S(1)}, u32[]{:S(2)}, u32[]{:S(2)}) %all-to-all-start.2) | async-done | bytes 2097184 | tf_op jit(solution)/shard_map/all_to_all | solution.py:222
  265.3 0.0 copy-start
  265.3 1.3 copy-done
  266.6 4.8 %z_inverse.3 = f32[2048,256]{1,0:T(8,128)} custom-call(f32[4096,128]{1,0:T(8,128)} %bitcast.14, bf16[256,256]{1,0:T(8,128)(2,1)} %constant.32.clone.refs_1_.h_ref, bf16[256,256]{1,0:T(8,128)(2,1)} %constant.33.clone.refs_2_.l_ref, f32[2048,256]{1,0:T(8,128)} %z_inverse.2.rest_0_), custom_call_target="tpu_custom_call" | custom-call | flops 805306368 | bytes 4194304 | tf_op jit(solution)/shard_map/z_inverse/pallas_call | solution.py:108
Async XLA Ops:
  6.4 99.2 %all-to-all-start.1 = ((f32[32,256,128]{2,1,0:T(8,128)}), f32[32,256,128]{2,1,0:T(8,128)}, u32[]{:S(2)}, u32[]{:S(2)}) async-start(f32[32,256,128]{2,1,0:T(8,128)} %bitcast.11), calls=%async_computation.1 | async-start | bytes 8388608 | tf_op jit(solution)/shard_map/all_to_all | solution.py:222
  105.6 54.1 %all-to-all-start = ((f32[32,128,128]{2,1,0:T(8,128)}), f32[32,128,128]{2,1,0:T(8,128)S(1)}, u32[]{:S(2)}, u32[]{:S(2)}) async-start(f32[32,128,128]{2,1,0:T(8,128)} %bitcast.16), calls=%async_computation | async-start | bytes 4194304 | tf_op jit(solution)/shard_map/all_to_all | solution.py:222
  159.7 1.3 copy-start.2
  161.0 51.5 %all-to-all-start.3 = ((f32[32,128,128]{2,1,0:T(8,128)}), f32[32,128,128]{2,1,0:T(8,128)S(1)}, u32[]{:S(2)}, u32[]{:S(2)}) async-start(f32[32,128,128]{2,1,0:T(8,128)} %bitcast.20), calls=%async_computation.3 | async-start | bytes 4194304 | tf_op jit(solution)/shard_map/all_to_all | solution.py:222
  212.5 1.3 copy-start.1
  213.8 51.5 %all-to-all-start.2 = ((f32[32,128,128]{2,1,0:T(8,128)}), f32[32,128,128]{2,1,0:T(8,128)S(1)}, u32[]{:S(2)}, u32[]{:S(2)}) async-start(f32[32,128,128]{2,1,0:T(8,128)} %bitcast.19), calls=%async_computation.2 | async-start | bytes 4194304 | tf_op jit(solution)/shard_map/all_to_all | solution.py:222
  265.3 1.3 copy-start

commit v3 on v2

v3 whole, which is shorter than its diff:
```python
import numpy as np
import jax
import jax.numpy as jnp
from jax import lax
from jax.experimental import pallas as pl
from jax.experimental.pallas import tpu as pltpu
from jax.sharding import PartitionSpec as P


ALL = ("row", "col")
LANES = 128
BF16 = jnp.bfloat16
F32 = jnp.float32
NN = (((1,), (0,)), ((), ()))
NT = (((1,), (1,)), ((), ()))
TN = (((0,), (0,)), ((), ()))


def split_table(table):
    high = table.astype(np.float32).astype(jnp.bfloat16)
    low = (table - high.astype(np.float64)).astype(np.float32).astype(jnp.bfloat16)
    return high, low


def wave_tables(extent):
    freqs = np.arange(extent)[:, None] + 0.5
    cells = np.arange(extent)[None, :]
    angles = np.pi / extent * freqs * (cells - (extent - 1) / 2)
    waves = np.concatenate([np.cos(angles), np.sin(angles)], axis=0)
    weights = np.where(cells == 0, 1.0, 2.0)
    even = weights * np.cos(np.pi / extent * freqs * cells)
    return waves, even


def split(value):
    high = value.astype(BF16)
    low = (value - high.astype(F32)).astype(BF16)
    return high, low


def stack_left(high, low, axis):
    return jnp.concatenate([high, high, low], axis=axis)


def stack_right(high, low, axis):
    return jnp.concatenate([high, low, high], axis=axis)


def dot(left, right, dims):
    return lax.dot_general(left, right, dims, preferred_element_type=F32)


def whole(shape):
    return pl.BlockSpec(shape, lambda *_: (0,) * len(shape))


def z_forward(sources, n_dev, pairs):
    rows, extent = sources[0][0].shape
    planes = extent // n_dev
    width = planes * len(sources)
    per = min(8, pairs)
    n = len(sources)

    def body(*refs):
        out_ref = refs[-1]
        step = pl.program_id(0)
        for g in range(n):
            x_ref, h_ref, l_ref = refs[3 * g : 3 * g + 3]
            right = stack_right(*split(x_ref[...]), 1)
            part = slice(sources[g][3], sources[g][3] + extent)
            acc = dot(stack_left(h_ref[part, :], l_ref[part, :], 1), right, NT)
            for h in range(per):
                for d in range(n_dev):
                    start = (d * width + g * planes) * pairs + per * step + h
                    out_ref[pl.ds(start, planes, stride=pairs), :] = acc[
                        d * planes : (d + 1) * planes, h * LANES : (h + 1) * LANES
                    ]

    lines = pl.BlockSpec((per * LANES, extent), lambda i: (i, 0))
    return pl.pallas_call(
        body,
        grid=(pairs // per,),
        in_specs=[s for source in sources for s in (lines, whole(source[1].shape), whole(source[2].shape))],
        out_specs=whole((n_dev * width * pairs, LANES)),
        out_shape=jax.ShapeDtypeStruct((n_dev * width * pairs, LANES), F32),
        cost_estimate=pl.CostEstimate(flops=6 * rows * extent * extent * n, transcendentals=0, bytes_accessed=8 * rows * extent * n),
        name="z_forward",
    )(*[a for source in sources for a in source[:3]])


SCALAR = pl.BlockSpec(memory_space=pltpu.SMEM)
VECTOR = pl.BlockSpec(memory_space=pltpu.VMEM)


def z_inverse(col, received, tables, table_rows, pairs, extent, partial):
    rows = pairs * LANES
    per = min(8, pairs)
    first, last = table_rows
    n_col = tables[0].shape[0]
    n_row = received[-1].shape[0]
    planes = (last - first) // n_row
    received = [r.reshape(-1, LANES) for r in received]

    def body(col_ref, *refs):
        r_refs = refs[: len(received)]
        h_ref, l_ref, *rest = refs[len(received) :]
        out_ref = rest[-1]
        step = pl.program_id(0)

        def block(h, s, j):
            start = j * pairs + per * step + h
            if s > 0 and len(r_refs) > 1:
                return r_refs[s][pl.ds(start, n_row, stride=planes * pairs), :]
            return r_refs[0][pl.ds(s * planes * pairs + start, n_row, stride=n_col * planes * pairs), :]

        left = jnp.concatenate(
            [
                jnp.concatenate([block(h, s, j) for s in range(n_col) for j in range(planes)], axis=0)
                for h in range(per)
            ],
            axis=1,
        )
        source = [lax.rem(col_ref[0] + n_col - s, n_col) for s in range(n_col)]
        high = jnp.concatenate([h_ref[c, first:last] for c in source], axis=0)
        low = jnp.concatenate([l_ref[c, first:last] for c in source], axis=0)
        acc = dot(stack_right(*split(left), 0), stack_left(high, low, 0), TN)
        if partial is not None:
            acc = acc + rest[0][...]
        out_ref[...] = acc

    lines = pl.BlockSpec((per * LANES, extent), lambda i: (i, 0))
    extra = [] if partial is None else [partial]
    return pl.pallas_call(
        body,
        grid=(pairs // per,),
        in_specs=[SCALAR] + [VECTOR] * len(received) + [whole(t.shape) for t in tables] + [lines] * len(extra),
        out_specs=lines,
        out_shape=jax.ShapeDtypeStruct((rows, extent), F32),
        cost_estimate=pl.CostEstimate(
            flops=6 * rows * extent * n_col * (last - first), transcendentals=0, bytes_accessed=8 * rows * extent
        ),
        name="z_inverse",
    )(col, *received, *tables, *extra)


def lane_half(shape):
    return lax.broadcasted_iota(jnp.int32, shape, 1) < LANES // 2


def swap(value):
    return pltpu.roll(value, LANES // 2, 1)


def read_plane(ref, index, plane_ref):
    n_row, n_col, _, pairs, _ = ref.shape
    half_x = n_row * pairs
    mask = lane_half((half_x, LANES))
    for p in range(n_col // 2):
        a = ref[:, 2 * p, index].reshape(half_x, LANES)
        b = ref[:, 2 * p + 1, index].reshape(half_x, LANES)
        plane_ref[p, pl.ds(0, half_x, stride=2)] = jnp.where(mask, a, swap(b))
        plane_ref[p, pl.ds(1, half_x, stride=2)] = jnp.where(mask, swap(a), b)
    return jnp.concatenate([plane_ref[p] for p in range(n_col // 2)], axis=1)


def write_plane(col, plane, plane_ref, block_ref, store):
    n_col = block_ref.shape[0]
    half_x = plane_ref.shape[1] // 2
    mask = lane_half((half_x, LANES))
    for p in range(n_col // 2):
        plane_ref[p] = plane[:, p * LANES : (p + 1) * LANES]
        q0 = plane_ref[p, pl.ds(0, half_x, stride=2)]
        q1 = plane_ref[p, pl.ds(1, half_x, stride=2)]
        block_ref[2 * p] = jnp.where(mask, q0, swap(q1))
        block_ref[2 * p + 1] = jnp.where(mask, swap(q0), q1)
    for s in range(n_col):
        store(s, block_ref[lax.rem(col + s, n_col)])


def kernel_planes(received, planes, tables, extent):
    scaling = 1.0 / float(extent) ** 3

    def body(r_ref, yh, yl, out_ref, plane_ref):
        plane = read_plane(r_ref, pl.program_id(0), plane_ref)
        first = dot(stack_left(yh[...], yl[...], 1), stack_right(*split(plane), 0), NN)
        second = dot(stack_left(*split(first), 1), stack_right(yh[...], yl[...], 1), NT)
        out_ref[0] = second * scaling

    return pl.pallas_call(
        body,
        grid=(planes,),
        in_specs=[VECTOR] + [whole(t.shape) for t in tables],
        out_specs=pl.BlockSpec((1, extent, extent), lambda k: (k, 0, 0)),
        out_shape=jax.ShapeDtypeStruct((planes, extent, extent), F32),
        scratch_shapes=[pltpu.VMEM((extent // LANES, extent, LANES), F32)],
        cost_estimate=pl.CostEstimate(flops=12 * planes * extent**3, transcendentals=0, bytes_accessed=8 * planes * extent**2),
        name="kernel_planes",
    )(received, *tables)


def convolve_planes(col, received, offset, kernel, kernel_offset, planes, joined, t_tables, y_tables, extent):
    n_row, n_col, _, pairs, _ = received.shape

    def body(col_ref, r_ref, k_ref, th, tl, yh, yl, *rest):
        *outs, plane_ref, block_ref = rest
        plane = read_plane(r_ref, offset + pl.program_id(0), plane_ref)
        along_x = dot(stack_left(yh[...], yl[...], 1), stack_right(*split(plane), 0), NN)
        spectrum = dot(stack_left(*split(along_x), 1), stack_right(yh[...], yl[...], 1), NT)
        weight = k_ref[0]
        weight = jnp.concatenate([weight, weight], axis=1)
        spectrum = spectrum * jnp.concatenate([weight, weight], axis=0)
        along_y = dot(stack_left(*split(spectrum), 1), stack_right(yh[...], yl[...], 0), NN)
        result = dot(stack_left(th[...], tl[...], 1), stack_right(*split(along_y), 0), NN)

        def store(s, value):
            value = value.reshape(n_row, pairs, LANES)
            if joined:
                outs[0][:, s, 0] = value
            else:
                outs[s][:, 0] = value

        write_plane(col_ref[0], result, plane_ref, block_ref, store)

    tables = (*t_tables, *y_tables)
    if joined:
        shapes = [(n_row, n_col, planes, pairs, LANES)]
        specs = [pl.BlockSpec((n_row, n_col, 1, pairs, LANES), lambda k: (0, 0, k, 0, 0))]
    else:
        shapes = [(n_row, planes, pairs, LANES)] * n_col
        specs = [pl.BlockSpec((n_row, 1, pairs, LANES), lambda k: (0, k, 0, 0))] * n_col
    return pl.pallas_call(
        body,
        grid=(planes,),
        in_specs=[SCALAR, VECTOR, pl.BlockSpec((1, extent, extent), lambda k: (kernel_offset + k, 0, 0))]
        + [whole(t.shape) for t in tables],
        out_specs=specs,
        out_shape=[jax.ShapeDtypeStruct(s, F32) for s in shapes],
        scratch_shapes=[
            pltpu.VMEM((extent // LANES, extent, LANES), F32),
            pltpu.VMEM((n_col, n_row * pairs, LANES), F32),
        ],
        cost_estimate=pl.CostEstimate(flops=72 * planes * extent**3, transcendentals=0, bytes_accessed=12 * planes * extent**2),
        name="convolve_planes",
    )(col, received, kernel, *tables)


def join(parts):
    n_row, length, _ = parts[0].shape
    block = n_row // 2

    def body(*refs):
        for s, ref in enumerate(refs[:-1]):
            refs[-1][:, s] = ref[...]

    return pl.pallas_call(
        body,
        grid=(n_row // block,),
        in_specs=[pl.BlockSpec((block, length, LANES), lambda i: (i, 0, 0))] * len(parts),
        out_specs=pl.BlockSpec((block, len(parts), length, LANES), lambda i: (i, 0, 0, 0)),
        out_shape=jax.ShapeDtypeStruct((n_row, len(parts), length, LANES), F32),
        name="join",
    )(*parts)


def solution(mesh):
    n_row, n_col = mesh.shape["row"], mesh.shape["col"]
    n_dev = n_row * n_col

    def on_device(density, green_octant):
        local_x, local_y, extent = density.shape
        pairs = local_x * local_y // LANES
        freqs = extent // n_dev
        waves, even = wave_tables(extent)
        y_waves = split_table(waves)
        t_waves = split_table(waves.T)
        y_even = split_table(even)

        def by_owner(table):
            table = table.reshape(n_row, n_col, freqs, extent).transpose(1, 2, 0, 3)
            return table.reshape(n_col, freqs * n_row, extent)

        cos_z = split_table(by_owner(waves[:extent]))
        sin_z = split_table(by_owner(waves[extent:]))
        col = lax.axis_index("col").astype(jnp.int32).reshape(1)

        def exchange(value):
            value = lax.all_to_all(value.reshape(n_dev, -1, LANES), ALL, 0, 0)
            return value.reshape(n_row, n_col, -1, pairs, LANES)

        def spread(value):
            return lax.all_to_all(value.reshape(n_row, n_col, -1, LANES), "row", 0, 0)

        def send(values):
            received = []
            for s, value in enumerate(values, start=1):
                perm = [(c, (c + s) % n_col) for c in range(n_col)]
                received.append(lax.ppermute(value.reshape(n_row, -1, LANES), "col", perm))
            return received

        dens = density.reshape(-1, extent)
        green = green_octant.reshape(-1, extent)
        first = exchange(z_forward([(green, *y_even, 0), (dens, *y_waves, 0)], n_dev, pairs))
        second = exchange(z_forward([(dens, *y_waves, extent)], n_dev, pairs))
        kernel = kernel_planes(first, freqs, y_even, extent)
        own, *others = convolve_planes(col, first, freqs, kernel, 0, freqs, False, t_waves, y_waves, extent)
        others = send(others)
        begin = freqs // 2
        parts = []
        for start, stop in ((0, begin), (begin, freqs)):
            (out,) = convolve_planes(col, second, start, kernel, start, stop - start, True, t_waves, y_waves, extent)
            out = spread(out)
            sent = send([out[:, s] for s in range(1, n_col)])
            parts.append(([out, *sent], (start * n_row, stop * n_row)))
        cos_b = join([own.reshape(n_row, -1, LANES), *others])
        cos_b = lax.all_to_all(cos_b, "row", 0, 0)
        result = z_inverse(col, parts[0][0], sin_z, parts[0][1], pairs, extent, None)
        result = z_inverse(col, [cos_b], cos_z, (0, freqs * n_row), pairs, extent, result)
        result = z_inverse(col, parts[1][0], sin_z, parts[1][1], pairs, extent, result)
        return result.reshape(local_x, local_y, extent)

    spec = P("row", "col", None)
    return jax.shard_map(on_device, mesh=mesh, in_specs=(spec, spec), out_specs=spec, check_vma=False)
```

time: 272 us -> 332 us (1.22)
  starting transfers between devices: 19.3 us -> 48.5 us
  waiting for transfers between devices: 174 us -> 191 us
  Pallas kernels: 73.8 us -> 83.9 us
  local copies, waits for them, and re-layouts: 3.97 us -> 7.5 us
    ppermute x0 -> x9, waiting for transfers between devices: none -> 63.7 us  [send(): received.append(lax.ppermute(value.reshape(n_row, -1, LANES), 'col', perm))]
    all_to_all x4 -> x5, waiting for transfers between devices: 174 us -> 127 us  [the longest x2 127 us: exchange(): value = lax.all_to_all(value.reshape(n_dev, -1, LANES), ALL, 0, 0)]
    ppermute x0 -> x9, starting transfers between devices: none -> 21.9 us  [send(): received.append(lax.ppermute(value.reshape(n_row, -1, LANES), 'col', perm))]
    pallas_call x7 -> x10, Pallas kernels: 73.8 us -> 83.9 us  [the longest x3 49 us: convolve_planes(): pl.pallas_call(body, grid=(planes,), in_specs=[SCALAR, VECTOR, pl.BlockSp...]
    all_to_all x4 -> x5, starting transfers between devices: 19.3 us -> 26.5 us  [the longest x2 13 us: exchange(): value = lax.all_to_all(value.reshape(n_dev, -1, LANES), ALL, 0, 0)]
  transfers between devices with their start and end apart: 4 -> 14, of which waited for: 4 -> 7; matrix products, arithmetic and copies ran while one was open for 0% -> 1% of each run, Pallas kernels for 23% -> 18%
where the time goes in v3:
time: 332 us; the launch traced here: 331 us
  waiting for transfers between devices  191 us (58%)
  Pallas kernels  83.9 us (25%)
  starting transfers between devices  48.5 us (15%)
  local copies, waits for them, and re-layouts  7.5 us (2%)
    all_to_all x2, waiting for transfers between devices, exchange(): value = lax.all_to_all(value.reshape(n_dev, -1, LANES), ALL, 0, 0)  127 us
    ppermute x9, waiting for transfers between devices, send(): received.append(lax.ppermute(value.reshape(n_row, -1, LANES), 'col', perm))  63.7 us
    pallas_call x3, Pallas kernels, convolve_planes(): pl.pallas_call(body, grid=(planes,), in_specs=[SCALAR, VECTOR, pl.BlockSp...  49 us
    ppermute x9, starting transfers between devices, send(): received.append(lax.ppermute(value.reshape(n_row, -1, LANES), 'col', perm))  21.9 us
    all_to_all x2, starting transfers between devices, exchange(): value = lax.all_to_all(value.reshape(n_dev, -1, LANES), ALL, 0, 0)  13 us
    pallas_call x3, Pallas kernels, z_inverse(): pl.pallas_call(body, grid=(pairs // per,), in_specs=[SCALAR] + [VECTOR] *...  12.6 us
    pallas_call x2, Pallas kernels, z_forward(): pl.pallas_call(body, grid=(pairs // per,), in_specs=[s for source in sour...  10.8 us
    all_to_all x2, starting transfers between devices, spread(): return lax.all_to_all(value.reshape(n_row, n_col, -1, LANES), 'row', 0, 0)  9.13 us
  transfers between devices with their start and end apart: 14, of which 7 were waited for; matrix products, arithmetic and copies ran while one was open for 1% of the time, Pallas kernels for 18%

profile of v3, /device:TPU:1, one launch (start us, length us, event | category | flops | bytes accessed | tf_op | source)
XLA Modules:
  0.0 330.8 jit_solution(2959019181477970309)
XLA Ops:
  0.0 6.5 %z_forward.3 = f32[8192,128]{1,0:T(8,128)} custom-call(f32[2048,256]{1,0:T(8,128)} %bitcast.44, bf16[256,256]{1,0:T(8,128)(2,1)} %constant.24.clone.refs_1_.yh, bf16[256,256]{1,0:T(8,128)(2,1)} %constant.25.clone.refs_2_.yl, f32[2048,256]{1,0:T(8,128)} %bitcast.38, bf16[512,256]{1,0:T(8,128)(2,1)} %constant.26.clone.refs_1_.refs_4_.yh, ...), custom_call_target="tpu_custom_call" | custom-call | flops 1610612736 | bytes 8388608 | tf_op jit(solution)/shard_map/z_forward/pallas_call | solution.py:80
  6.5 7.1 %all-to-all-start.1 = ((f32[32,256,128]{2,1,0:T(8,128)}), f32[32,256,128]{2,1,0:T(8,128)}, u32[]{:S(2)}, u32[]{:S(2)}) async-start(f32[32,256,128]{2,1,0:T(8,128)} %bitcast.35), calls=%async_computation.1 | async-start | bytes 8388608 | tf_op jit(solution)/shard_map/all_to_all | solution.py:287
  13.7 4.2 %z_forward.2 = f32[4096,128]{1,0:T(8,128)} custom-call(f32[2048,256]{1,0:T(8,128)} %bitcast.39, bf16[512,256]{1,0:T(8,128)(2,1)} %constant.26.clone.refs_1_.refs_4_.yh, bf16[512,256]{1,0:T(8,128)(2,1)} %constant.27.clone.refs_2_.refs_5_.yl), custom_call_target="tpu_custom_call" | custom-call | flops 805306368 | bytes 4194304 | tf_op jit(solution)/shard_map/z_forward/pallas_call | solution.py:80
  17.9 87.8 %all-to-all-done.1 = f32[32,256,128]{2,1,0:T(8,128)} async-done(((f32[32,256,128]{2,1,0:T(8,128)}), f32[32,256,128]{2,1,0:T(8,128)}, u32[]{:S(2)}, u32[]{:S(2)}) %all-to-all-start.1) | async-done | bytes 4194336 | tf_op jit(solution)/shard_map/all_to_all | solution.py:287
  105.7 5.8 %all-to-all-start = ((f32[32,128,128]{2,1,0:T(8,128)}), f32[32,128,128]{2,1,0:T(8,128)S(1)}, u32[]{:S(2)}, u32[]{:S(2)}) async-start(f32[32,128,128]{2,1,0:T(8,128)} %bitcast.37), calls=%async_computation | async-start | bytes 4194304 | tf_op jit(solution)/shard_map/all_to_all | solution.py:287
  111.5 9.0 %kernel_planes.1.k_ref = f32[8,256,256]{2,1,0:T(8,128)} custom-call(f32[8,4,16,16,128]{4,3,2,1,0:T(8,128)} %bitcast.6.r_ref, bf16[256,256]{1,0:T(8,128)(2,1)} %constant.24.clone.refs_1_.yh, bf16[256,256]{1,0:T(8,128)(2,1)} %constant.25.clone.refs_2_.yl), custom_call_target="tpu_custom_call" | custom-call | flops 1610612736 | bytes 4194304 | tf_op jit(solution)/shard_map/kernel_planes/pallas_call | solution.py:189
  120.5 39.3 %all-to-all-done = f32[32,128,128]{2,1,0:T(8,128)S(1)} async-done(((f32[32,128,128]{2,1,0:T(8,128)}), f32[32,128,128]{2,1,0:T(8,128)S(1)}, u32[]{:S(2)}, u32[]{:S(2)}) %all-to-all-start) | async-done | bytes 2097184 | tf_op jit(solution)/shard_map/all_to_all | solution.py:287
  159.8 1.3 copy-done.3
  161.1 12.8 %convolve_planes.5 = f32[8,4,4,16,128]{4,3,2,1,0:T(8,128)} custom-call(s32[1]{0:T(128)} %bitcast.col_ref, f32[8,4,8,16,128]{4,3,2,1,0:T(8,128)} %bitcast.42, f32[8,256,256]{2,1,0:T(8,128)} %kernel_planes.1.k_ref, bf16[256,512]{1,0:T(8,128)(2,1)} %constant.28.clone.th, bf16[256,512]{1,0:T(8,128)(2,1)} %constant.29.clone.tl, ...), custom_call_target="tpu_custom_call" | custom-call | flops 4831838208 | bytes 3145728 | tf_op jit(solution)/shard_map/convolve_planes/pallas_call | solution.py:231
  173.9 3.5 %all-to-all-start.4 = ((f32[8,4,64,128]{3,2,1,0:T(8,128)}), f32[8,4,64,128]{3,2,1,0:T(8,128)S(1)}, u32[]{:S(2)}, u32[]{:S(2)}) async-start(f32[8,4,64,128]{3,2,1,0:T(8,128)} %bitcast.46), calls=%async_computation.4 | async-start | bytes 2097152 | tf_op jit(solution)/shard_map/all_to_all | solution.py:291
  177.4 12.8 %convolve_planes.3 = f32[8,4,4,16,128]{4,3,2,1,0:T(8,128)} custom-call(s32[1]{0:T(128)} %bitcast.col_ref, f32[8,4,8,16,128]{4,3,2,1,0:T(8,128)} %bitcast.43, f32[8,256,256]{2,1,0:T(8,128)} %kernel_planes.1.k_ref, bf16[256,512]{1,0:T(8,128)(2,1)} %constant.28.clone.th, bf16[256,512]{1,0:T(8,128)(2,1)} %constant.29.clone.tl, ...), custom_call_target="tpu_custom_call" | custom-call | flops 4831838208 | bytes 3145728 | tf_op jit(solution)/shard_map/convolve_planes/pallas_call | solution.py:231
  190.2 1.0 copy-done.2
  191.2 5.6 %all-to-all-start.2 = ((f32[8,4,64,128]{3,2,1,0:T(8,128)}), f32[8,4,64,128]{3,2,1,0:T(8,128)S(1)}, u32[]{:S(2)}, u32[]{:S(2)}) async-start(f32[8,4,64,128]{3,2,1,0:T(8,128)} %bitcast.45), calls=%async_computation.2 | async-start | bytes 2097152 | tf_op jit(solution)/shard_map/all_to_all | solution.py:291
  196.8 23.5 %convolve_planes.4 = (f32[8,8,16,128]{3,2,1,0:T(8,128)}, f32[8,8,16,128]{3,2,1,0:T(8,128)}, f32[8,8,16,128]{3,2,1,0:T(8,128)}, f32[8,8,16,128]{3,2,1,0:T(8,128)}) custom-call(s32[1]{0:T(128)} %bitcast.col_ref, f32[8,4,16,16,128]{4,3,2,1,0:T(8,128)} %bitcast.6.r_ref, f32[8,256,256]{2,1,0:T(8,128)} %kernel_planes.1.k_ref, bf16[256,512]{1,0:T(8,128)(2,1)} %constant.28.clone.th, ...), custom_call_target="tpu_custom_call" | custom-call | flops 9663676416 | bytes 6291456 | tf_op jit(solution)/shard_map/convolve_planes/pallas_call | solution.py:231
  220.3 2.6 collective-permute-start.3
  223.0 2.1 collective-permute-start.5
  225.0 10.7 %collective-permute-done.3.refs_1_ = f32[8,128,128]{2,1,0:T(8,128)S(1)} collective-permute-done((f32[8,128,128]{2,1,0:T(8,128)}, f32[8,128,128]{2,1,0:T(8,128)S(1)}, u32[]{:S(2)}, u32[]{:S(2)}) %collective-permute-start.3) | collective-permute-done | bytes 524320 | tf_op jit(solution)/shard_map/ppermute | solution.py:297
  235.8 22.9 %collective-permute-done.4.refs_2_ = f32[8,128,128]{2,1,0:T(8,128)S(1)} collective-permute-done((f32[8,128,128]{2,1,0:T(8,128)}, f32[8,128,128]{2,1,0:T(8,128)S(1)}, u32[]{:S(2)}, u32[]{:S(2)}) %collective-permute-start.4) | collective-permute-done | bytes 524320 | tf_op jit(solution)/shard_map/ppermute | solution.py:297
  258.7 0.8 copy-done.5
  259.7 2.6 join.1
  262.3 4.4 %all-to-all-start.3 = ((f32[8,4,128,128]{3,2,1,0:T(8,128)}), f32[8,4,128,128]{3,2,1,0:T(8,128)S(1)}, u32[]{:S(2)}, u32[]{:S(2)}) async-start(f32[8,4,128,128]{3,2,1,0:T(8,128)} %join.1), calls=%async_computation.3 | async-start | bytes 4194304 | tf_op jit(solution)/shard_map/all_to_all | solution.py:315
  266.7 1.2 slice_bitcast_fusion
  267.9 12.6 %collective-permute-start.8 = (f32[8,64,128]{2,1,0:T(8,128)S(1)}, f32[8,64,128]{2,1,0:T(8,128)S(1)}, u32[]{:S(2)}, u32[]{:S(2)}) collective-permute-start(f32[8,64,128]{2,1,0:T(8,128)S(1)} %get-tuple-element.13), channel_id=1, source_target_pairs={{0,3},{1,0},{2,1},{3,2},{4,7},{5,4},{6,5},{7,6},{8,11},{9,8},{10,9... | collective-permute-start | bytes 786440 | tf_op jit(solution)/shard_map/ppermute | solution.py:297
  280.8 0.9 slice_bitcast_fusion.3
  281.7 2.9 collective-permute-start.2
  285.2 1.0 collective-permute-done.8
  287.0 16.7 %collective-permute-done.7 = f32[8,64,128]{2,1,0:T(8,128)} collective-permute-done((f32[8,64,128]{2,1,0:T(8,128)S(1)}, f32[8,64,128]{2,1,0:T(8,128)}, u32[]{:S(2)}, u32[]{:S(2)}) %collective-permute-start.7) | collective-permute-done | bytes 262176 | tf_op jit(solution)/shard_map/ppermute | solution.py:297
  303.7 3.6 %z_inverse.3.refs_3_ = f32[2048,256]{1,0:T(8,128)} custom-call(s32[1]{0:T(128)} %bitcast.col_ref, f32[2048,128]{1,0:T(8,128)} %bitcast.41, f32[512,128]{1,0:T(8,128)} %bitcast.23.refs_1_, f32[512,128]{1,0:T(8,128)} %bitcast.25.refs_2_, f32[512,128]{1,0:T(8,128)} %bitcast.51, bf16[4,64,256]{2,1,0:T(8,128)(2,1)} %constant.30.clone.refs_4_, ...), custom_call_target="tpu_custom_call" | custom-call | flops 402653184 | bytes 4194304 | tf_op jit(solution)/shard_map/z_inverse/pallas_call | solution.py:133
  307.3 1.3 copy-done
  308.6 5.0 %z_inverse.4.refs_6_ = f32[2048,256]{1,0:T(8,128)} custom-call(s32[1]{0:T(128)} %bitcast.col_ref, f32[4096,128]{1,0:T(8,128)} %bitcast.36, bf16[4,64,256]{2,1,0:T(8,128)(2,1)} %constant.32.clone.refs_1_, bf16[4,64,256]{2,1,0:T(8,128)(2,1)} %constant.33.clone.refs_2_, f32[2048,256]{1,0:T(8,128)} %z_inverse.3.refs_3_), custom_call_target="tpu_custom_call" | custom-call | flops 805306368 | bytes 4194304 | tf_op jit(solution)/shard_map/z_inverse/pallas_call | solution.py:133
  313.6 12.4 %collective-permute-done.1 = f32[8,64,128]{2,1,0:T(8,128)S(1)} collective-permute-done((f32[8,64,128]{2,1,0:T(8,128)}, f32[8,64,128]{2,1,0:T(8,128)S(1)}, u32[]{:S(2)}, u32[]{:S(2)}) %collective-permute-start.1) | collective-permute-done | bytes 262176 | tf_op jit(solution)/shard_map/ppermute | solution.py:297
  326.8 4.0 %z_inverse.5 = f32[2048,256]{1,0:T(8,128)} custom-call(s32[1]{0:T(128)} %bitcast.col_ref, f32[2048,128]{1,0:T(8,128)} %bitcast.40, f32[512,128]{1,0:T(8,128)} %bitcast.50, f32[512,128]{1,0:T(8,128)} %bitcast.49, f32[512,128]{1,0:T(8,128)} %bitcast.48, bf16[4,64,256]{2,1,0:T(8,128)(2,1)} %constant.30.clone.refs_4_, ...), custom_call_target="tpu_custom_call" | custom-call | flops 402653184 | bytes 4194304 | tf_op jit(solution)/shard_map/z_inverse/pallas_call | solution.py:133
  (30 shorter events, 2.9 us)
Async XLA Ops:
  6.5 99.2 %all-to-all-start.1 = ((f32[32,256,128]{2,1,0:T(8,128)}), f32[32,256,128]{2,1,0:T(8,128)}, u32[]{:S(2)}, u32[]{:S(2)}) async-start(f32[32,256,128]{2,1,0:T(8,128)} %bitcast.35), calls=%async_computation.1 | async-start | bytes 8388608 | tf_op jit(solution)/shard_map/all_to_all | solution.py:287
  105.7 54.1 %all-to-all-start = ((f32[32,128,128]{2,1,0:T(8,128)}), f32[32,128,128]{2,1,0:T(8,128)S(1)}, u32[]{:S(2)}, u32[]{:S(2)}) async-start(f32[32,128,128]{2,1,0:T(8,128)} %bitcast.37), calls=%async_computation | async-start | bytes 4194304 | tf_op jit(solution)/shard_map/all_to_all | solution.py:287
  159.8 1.3 copy-start.3
  173.9 16.3 %all-to-all-start.4 = ((f32[8,4,64,128]{3,2,1,0:T(8,128)}), f32[8,4,64,128]{3,2,1,0:T(8,128)S(1)}, u32[]{:S(2)}, u32[]{:S(2)}) async-start(f32[8,4,64,128]{3,2,1,0:T(8,128)} %bitcast.46), calls=%async_computation.4 | async-start | bytes 2097152 | tf_op jit(solution)/shard_map/all_to_all | solution.py:291
  190.2 1.0 copy-start.2
  191.2 71.1 %all-to-all-start.2 = ((f32[8,4,64,128]{3,2,1,0:T(8,128)}), f32[8,4,64,128]{3,2,1,0:T(8,128)S(1)}, u32[]{:S(2)}, u32[]{:S(2)}) async-start(f32[8,4,64,128]{3,2,1,0:T(8,128)} %bitcast.45), calls=%async_computation.2 | async-start | bytes 2097152 | tf_op jit(solution)/shard_map/all_to_all | solution.py:291
  220.3 15.5 %collective-permute-start.3 = (f32[8,128,128]{2,1,0:T(8,128)}, f32[8,128,128]{2,1,0:T(8,128)S(1)}, u32[]{:S(2)}, u32[]{:S(2)}) collective-permute-start(f32[8,128,128]{2,1,0:T(8,128)} %bitcast.54), channel_id=1, source_target_pairs={{0,1},{1,2},{2,3},{3,0},{4,5},{5,6},{6,7},{7,4},{8,9},{9,10},{10,1... | collective-permute-start | bytes 1572872 | tf_op jit(solution)/shard_map/ppermute | solution.py:297
  222.9 35.8 %collective-permute-start.4 = (f32[8,128,128]{2,1,0:T(8,128)}, f32[8,128,128]{2,1,0:T(8,128)S(1)}, u32[]{:S(2)}, u32[]{:S(2)}) collective-permute-start(f32[8,128,128]{2,1,0:T(8,128)} %bitcast.53), channel_id=1, source_target_pairs={{0,2},{1,3},{2,0},{3,1},{4,6},{5,7},{6,4},{7,5},{8,10},{9,11},{10,... | collective-permute-start | bytes 1572872 | tf_op jit(solution)/shard_map/ppermute | solution.py:297
  223.0 35.7 %collective-permute-start.5 = (f32[8,128,128]{2,1,0:T(8,128)}, f32[8,128,128]{2,1,0:T(8,128)S(1)}, u32[]{:S(2)}, u32[]{:S(2)}) collective-permute-start(f32[8,128,128]{2,1,0:T(8,128)} %bitcast.52), channel_id=1, source_target_pairs={{0,3},{1,0},{2,1},{3,2},{4,7},{5,4},{6,5},{7,6},{8,11},{9,8},{10,9... | collective-permute-start | bytes 1572872 | tf_op jit(solution)/shard_map/ppermute | solution.py:297
  235.8 22.9 %copy-start.4 = (f32[8,128,128]{2,1,0:T(8,128)}, f32[8,128,128]{2,1,0:T(8,128)S(1)}, u32[]{:S(2)}) copy-start(f32[8,128,128]{2,1,0:T(8,128)S(1)} %collective-permute-done.3.refs_1_) | copy-start | bytes 1572868
  258.7 0.8 copy-start.5
  258.7 1.0 copy-start.6
  262.3 18.5 %copy-start.1 = (f32[8,4,64,128]{3,2,1,0:T(8,128)}, f32[8,4,64,128]{3,2,1,0:T(8,128)S(1)}, u32[]{:S(2)}) copy-start(f32[8,4,64,128]{3,2,1,0:T(8,128)S(1)} %all-to-all-done.2) | copy-start | bytes 3145732
  262.3 45.0 %all-to-all-start.3 = ((f32[8,4,128,128]{3,2,1,0:T(8,128)}), f32[8,4,128,128]{3,2,1,0:T(8,128)S(1)}, u32[]{:S(2)}, u32[]{:S(2)}) async-start(f32[8,4,128,128]{3,2,1,0:T(8,128)} %join.1), calls=%async_computation.3 | async-start | bytes 4194304 | tf_op jit(solution)/shard_map/all_to_all | solution.py:315
  267.9 18.3 %collective-permute-start.8 = (f32[8,64,128]{2,1,0:T(8,128)S(1)}, f32[8,64,128]{2,1,0:T(8,128)S(1)}, u32[]{:S(2)}, u32[]{:S(2)}) collective-permute-start(f32[8,64,128]{2,1,0:T(8,128)S(1)} %get-tuple-element.13), channel_id=1, source_target_pairs={{0,3},{1,0},{2,1},{3,2},{4,7},{5,4},{6,5},{7,6},{8,11},{9,8},{10,9... | collective-permute-start | bytes 786440 | tf_op jit(solution)/shard_map/ppermute | solution.py:297
  280.4 23.2 %collective-permute-start.7 = (f32[8,64,128]{2,1,0:T(8,128)S(1)}, f32[8,64,128]{2,1,0:T(8,128)}, u32[]{:S(2)}, u32[]{:S(2)}) collective-permute-start(f32[8,64,128]{2,1,0:T(8,128)S(1)} %get-tuple-element.14), channel_id=1, source_target_pairs={{0,2},{1,3},{2,0},{3,1},{4,6},{5,7},{6,4},{7,5},{8,10},{9,11},{10,... | collective-permute-start | bytes 786440 | tf_op jit(solution)/shard_map/ppermute | solution.py:297
  280.4 23.2 %collective-permute-start.6 = (f32[8,64,128]{2,1,0:T(8,128)S(1)}, f32[8,64,128]{2,1,0:T(8,128)}, u32[]{:S(2)}, u32[]{:S(2)}) collective-permute-start(f32[8,64,128]{2,1,0:T(8,128)S(1)} %get-tuple-element.15), channel_id=1, source_target_pairs={{0,1},{1,2},{2,3},{3,0},{4,5},{5,6},{6,7},{7,4},{8,9},{9,10},{10,1... | collective-permute-start | bytes 786440 | tf_op jit(solution)/shard_map/ppermute | solution.py:297
  281.7 31.9 %collective-permute-start.2 = (f32[8,64,128]{2,1,0:T(8,128)}, f32[8,64,128]{2,1,0:T(8,128)S(1)}, u32[]{:S(2)}, u32[]{:S(2)}) collective-permute-start(f32[8,64,128]{2,1,0:T(8,128)} %get-tuple-element.16), channel_id=1, source_target_pairs={{0,3},{1,0},{2,1},{3,2},{4,7},{5,4},{6,5},{7,6},{8,11},{9,8},{10,9... | collective-permute-start | bytes 786440 | tf_op jit(solution)/shard_map/ppermute | solution.py:297
  284.6 41.4 %collective-permute-start.1 = (f32[8,64,128]{2,1,0:T(8,128)}, f32[8,64,128]{2,1,0:T(8,128)S(1)}, u32[]{:S(2)}, u32[]{:S(2)}) collective-permute-start(f32[8,64,128]{2,1,0:T(8,128)} %get-tuple-element.17), channel_id=1, source_target_pairs={{0,2},{1,3},{2,0},{3,1},{4,6},{5,7},{6,4},{7,5},{8,10},{9,11},{10,... | collective-permute-start | bytes 786440 | tf_op jit(solution)/shard_map/ppermute | solution.py:297
  286.2 17.5 %copy-start.10 = (f32[8,64,128]{2,1,0:T(8,128)}, f32[8,64,128]{2,1,0:T(8,128)S(1)}, u32[]{:S(2)}) copy-start(f32[8,64,128]{2,1,0:T(8,128)S(1)} %collective-permute-done.8) | copy-start | bytes 786436
  286.2 39.8 %collective-permute-start = (f32[8,64,128]{2,1,0:T(8,128)}, f32[8,64,128]{2,1,0:T(8,128)S(1)}, u32[]{:S(2)}, u32[]{:S(2)}) collective-permute-start(f32[8,64,128]{2,1,0:T(8,128)} %get-tuple-element.18), channel_id=1, source_target_pairs={{0,1},{1,2},{2,3},{3,0},{4,5},{5,6},{6,7},{7,4},{8,9},{9,10},{10,1... | collective-permute-start | bytes 786440 | tf_op jit(solution)/shard_map/ppermute | solution.py:297
  307.3 1.3 copy-start
  313.6 12.4 %copy-start.7 = (f32[8,64,128]{2,1,0:T(8,128)}, f32[8,64,128]{2,1,0:T(8,128)S(1)}, u32[]{:S(2)}) copy-start(f32[8,64,128]{2,1,0:T(8,128)S(1)} %collective-permute-done.2) | copy-start | bytes 786436
  326.0 0.7 copy-start.8
  326.0 0.8 copy-start.9

commit v4 on v3

v4 whole, which is shorter than its diff:
```python
import numpy as np
import jax
import jax.numpy as jnp
from jax import lax
from jax.experimental import pallas as pl
from jax.experimental.pallas import tpu as pltpu
from jax.sharding import PartitionSpec as P


ALL = ("row", "col")
LANES = 128
BF16 = jnp.bfloat16
F32 = jnp.float32
NN = (((1,), (0,)), ((), ()))
NT = (((1,), (1,)), ((), ()))
TN = (((0,), (0,)), ((), ()))


def split_table(table):
    high = table.astype(np.float32).astype(jnp.bfloat16)
    low = (table - high.astype(np.float64)).astype(np.float32).astype(jnp.bfloat16)
    return high, low


def wave_tables(extent):
    freqs = np.arange(extent)[:, None] + 0.5
    cells = np.arange(extent)[None, :]
    angles = np.pi / extent * freqs * (cells - (extent - 1) / 2)
    waves = np.concatenate([np.cos(angles), np.sin(angles)], axis=0)
    weights = np.where(cells == 0, 1.0, 2.0)
    even = weights * np.cos(np.pi / extent * freqs * cells)
    return waves, even


def split(value):
    high = value.astype(BF16)
    low = (value - high.astype(F32)).astype(BF16)
    return high, low


def stack_left(high, low, axis):
    return jnp.concatenate([high, high, low], axis=axis)


def stack_right(high, low, axis):
    return jnp.concatenate([high, low, high], axis=axis)


def dot(left, right, dims):
    return lax.dot_general(left, right, dims, preferred_element_type=F32)


def whole(shape):
    return pl.BlockSpec(shape, lambda *_: (0,) * len(shape))


SCALAR = pl.BlockSpec(memory_space=pltpu.SMEM)
VECTOR = pl.BlockSpec(memory_space=pltpu.VMEM)


def z_forward(sources, n_dev, pairs):
    rows, extent = sources[0][0].shape
    all_planes = extent // n_dev
    counts = [source[4] for source in sources]
    width = sum(counts)
    per = min(8, pairs)
    n = len(sources)

    def body(*refs):
        out_ref = refs[-1]
        step = pl.program_id(0)
        for g in range(n):
            x_ref, h_ref, l_ref = refs[3 * g : 3 * g + 3]
            right = stack_right(*split(x_ref[...]), 1)
            part = slice(sources[g][3], sources[g][3] + extent)
            acc = dot(stack_left(h_ref[part, :], l_ref[part, :], 1), right, NT)
            for h in range(per):
                for d in range(n_dev):
                    start = (d * width + sum(counts[:g])) * pairs + per * step + h
                    out_ref[pl.ds(start, counts[g], stride=pairs), :] = acc[
                        d * all_planes : d * all_planes + counts[g], h * LANES : (h + 1) * LANES
                    ]

    lines = pl.BlockSpec((per * LANES, extent), lambda i: (i, 0))
    return pl.pallas_call(
        body,
        grid=(pairs // per,),
        in_specs=[s for source in sources for s in (lines, whole(source[1].shape), whole(source[2].shape))],
        out_specs=whole((n_dev * width * pairs, LANES)),
        out_shape=jax.ShapeDtypeStruct((n_dev * width * pairs, LANES), F32),
        cost_estimate=pl.CostEstimate(flops=6 * rows * extent * extent * n, transcendentals=0, bytes_accessed=8 * rows * extent * n),
        name="z_forward",
    )(*[a for source in sources for a in source[:3]])


def z_forward_slots(col, lines, tables, table_rows, n_row, pairs):
    rows, extent = lines.shape
    per = min(8, pairs)
    first, last = table_rows
    n_col = tables[0].shape[0]
    planes = (last - first) // n_row

    def body(col_ref, x_ref, h_ref, l_ref, *out_refs):
        step = pl.program_id(0)
        target = [lax.rem(col_ref[0] + s, n_col) for s in range(n_col)]
        high = jnp.concatenate([h_ref[c, first:last] for c in target], axis=0)
        low = jnp.concatenate([l_ref[c, first:last] for c in target], axis=0)
        acc = dot(stack_left(high, low, 1), stack_right(*split(x_ref[...]), 1), NT)
        for s, out_ref in enumerate(out_refs):
            for j in range(planes):
                row = (s * planes + j) * n_row
                for h in range(per):
                    start = j * pairs + per * step + h
                    out_ref[pl.ds(start, n_row, stride=planes * pairs), :] = acc[
                        row : row + n_row, h * LANES : (h + 1) * LANES
                    ]

    shape = (n_row * planes * pairs, LANES)
    return pl.pallas_call(
        body,
        grid=(pairs // per,),
        in_specs=[SCALAR, pl.BlockSpec((per * LANES, extent), lambda i: (i, 0))] + [whole(t.shape) for t in tables],
        out_specs=[whole(shape)] * n_col,
        out_shape=[jax.ShapeDtypeStruct(shape, F32)] * n_col,
        cost_estimate=pl.CostEstimate(
            flops=6 * rows * extent * n_col * (last - first), transcendentals=0, bytes_accessed=8 * rows * extent
        ),
        name="z_forward_slots",
    )(col, lines, *tables)


def z_inverse(col, groups, n_row, pairs, extent, partial):
    rows = pairs * LANES
    per = min(8, pairs)
    n_col = groups[0][1][0].shape[0]
    counts = [len(received) for received, _, _ in groups]
    depth = n_col * sum(last - first for _, _, (first, last) in groups)

    def body(col_ref, *refs):
        refs = list(refs)
        step = pl.program_id(0)
        source = [lax.rem(col_ref[0] + n_col - s, n_col) for s in range(n_col)]
        columns = [[] for _ in range(per)]
        highs, lows = [], []
        for g, (_, _, (first, last)) in enumerate(groups):
            r_refs = [refs.pop(0) for _ in range(counts[g])]
            h_ref, l_ref = refs.pop(0), refs.pop(0)
            planes = (last - first) // n_row
            for s in range(n_col):
                ref, slots, place = (r_refs[s], 1, 0) if s > 0 and len(r_refs) > 1 else (r_refs[0], n_col, s)
                for j in range(planes):
                    for h in range(per):
                        start = (place * planes + j) * pairs + per * step + h
                        columns[h].append(ref[pl.ds(start, n_row, stride=slots * planes * pairs), :])
                highs.append(h_ref[source[s], first:last])
                lows.append(l_ref[source[s], first:last])
        left = jnp.concatenate([jnp.concatenate(blocks, axis=0) for blocks in columns], axis=1)
        high = jnp.concatenate(highs, axis=0)
        low = jnp.concatenate(lows, axis=0)
        acc = dot(stack_right(*split(left), 0), stack_left(high, low, 0), TN)
        if partial is not None:
            acc = acc + refs[0][...]
        refs[-1][...] = acc

    lines = pl.BlockSpec((per * LANES, extent), lambda i: (i, 0))
    specs, operands = [SCALAR], [col]
    for received, tables, _ in groups:
        specs += [VECTOR] * len(received) + [whole(t.shape) for t in tables]
        operands += [r.reshape(-1, LANES) for r in received] + list(tables)
    if partial is not None:
        specs.append(lines)
        operands.append(partial)
    return pl.pallas_call(
        body,
        grid=(pairs // per,),
        in_specs=specs,
        out_specs=lines,
        out_shape=jax.ShapeDtypeStruct((rows, extent), F32),
        cost_estimate=pl.CostEstimate(
            flops=6 * rows * extent * depth, transcendentals=0, bytes_accessed=8 * rows * extent
        ),
        name="z_inverse",
    )(*operands)


def lane_half(shape):
    return lax.broadcasted_iota(jnp.int32, shape, 1) < LANES // 2


def swap(value):
    return pltpu.roll(value, LANES // 2, 1)


def read_plane(ref, index, plane_ref, slot=lambda c: c):
    n_row, n_col, _, pairs, _ = ref.shape
    half_x = n_row * pairs
    mask = lane_half((half_x, LANES))
    for p in range(n_col // 2):
        a = ref[:, slot(2 * p), index].reshape(half_x, LANES)
        b = ref[:, slot(2 * p + 1), index].reshape(half_x, LANES)
        plane_ref[p, pl.ds(0, half_x, stride=2)] = jnp.where(mask, a, swap(b))
        plane_ref[p, pl.ds(1, half_x, stride=2)] = jnp.where(mask, swap(a), b)
    return jnp.concatenate([plane_ref[p] for p in range(n_col // 2)], axis=1)


def write_plane(col, plane, plane_ref, block_ref, store):
    n_col = block_ref.shape[0]
    half_x = plane_ref.shape[1] // 2
    mask = lane_half((half_x, LANES))
    for p in range(n_col // 2):
        plane_ref[p] = plane[:, p * LANES : (p + 1) * LANES]
        q0 = plane_ref[p, pl.ds(0, half_x, stride=2)]
        q1 = plane_ref[p, pl.ds(1, half_x, stride=2)]
        block_ref[2 * p] = jnp.where(mask, q0, swap(q1))
        block_ref[2 * p + 1] = jnp.where(mask, swap(q0), q1)
    for s in range(n_col):
        store(s, block_ref[lax.rem(col + s, n_col)])


def kernel_planes(received, planes, tables, extent):
    scaling = 1.0 / float(extent) ** 3
    per = min(4, planes)

    def body(r_ref, yh, yl, out_ref, plane_ref):
        for i in range(per):
            plane = read_plane(r_ref, per * pl.program_id(0) + i, plane_ref.at[i])
            first = dot(stack_left(yh[...], yl[...], 1), stack_right(*split(plane), 0), NN)
            second = dot(stack_left(*split(first), 1), stack_right(yh[...], yl[...], 1), NT)
            out_ref[i] = second * scaling

    return pl.pallas_call(
        body,
        grid=(planes // per,),
        in_specs=[VECTOR] + [whole(t.shape) for t in tables],
        out_specs=pl.BlockSpec((per, extent, extent), lambda k: (k, 0, 0)),
        out_shape=jax.ShapeDtypeStruct((planes, extent, extent), F32),
        scratch_shapes=[pltpu.VMEM((per, extent // LANES, extent, LANES), F32)],
        cost_estimate=pl.CostEstimate(flops=12 * planes * extent**3, transcendentals=0, bytes_accessed=8 * planes * extent**2),
        name="kernel_planes",
    )(received, *tables)


def convolve_planes(col, received, relative, offset, kernel, kernel_offset, planes, joined, t_tables, y_tables, extent):
    n_row, n_col, _, pairs, _ = received.shape

    per = 2 if planes % 2 == 0 else 1

    def body(col_ref, r_ref, k_ref, th, tl, yh, yl, *rest):
        *outs, plane_ref, block_ref = rest
        slot = (lambda c: lax.rem(col_ref[0] + (n_col - c), n_col)) if relative else (lambda c: c)
        results = []
        for i in range(per):
            plane = read_plane(r_ref, offset + per * pl.program_id(0) + i, plane_ref.at[i], slot)
            along_x = dot(stack_left(yh[...], yl[...], 1), stack_right(*split(plane), 0), NN)
            weight = jnp.concatenate([k_ref[i], k_ref[i]], axis=1)
            along_y = []
            for part in (along_x[:extent], along_x[extent:]):
                spectrum = dot(stack_left(*split(part), 1), stack_right(yh[...], yl[...], 1), NT) * weight
                along_y.append(dot(stack_left(*split(spectrum), 1), stack_right(yh[...], yl[...], 0), NN))
            along_y = jnp.concatenate(along_y, axis=0)
            results.append(dot(stack_left(th[...], tl[...], 1), stack_right(*split(along_y), 0), NN))

        for i in range(per):

            def store(s, value):
                value = value.reshape(n_row, pairs, LANES)
                if joined:
                    outs[0][:, s, i] = value
                else:
                    outs[s][:, i] = value

            write_plane(col_ref[0], results[i], plane_ref.at[i], block_ref, store)

    tables = (*t_tables, *y_tables)
    if joined:
        shapes = [(n_row, n_col, planes, pairs, LANES)]
        specs = [pl.BlockSpec((n_row, n_col, per, pairs, LANES), lambda k: (0, 0, k, 0, 0))]
    else:
        shapes = [(n_row, planes, pairs, LANES)] * n_col
        specs = [pl.BlockSpec((n_row, per, pairs, LANES), lambda k: (0, k, 0, 0))] * n_col
    return pl.pallas_call(
        body,
        grid=(planes // per,),
        in_specs=[SCALAR, VECTOR, pl.BlockSpec((per, extent, extent), lambda k: (kernel_offset // per + k, 0, 0))]
        + [whole(t.shape) for t in tables],
        out_specs=specs,
        out_shape=[jax.ShapeDtypeStruct(s, F32) for s in shapes],
        scratch_shapes=[
            pltpu.VMEM((per, extent // LANES, extent, LANES), F32),
            pltpu.VMEM((n_col, n_row * pairs, LANES), F32),
        ],
        cost_estimate=pl.CostEstimate(flops=72 * planes * extent**3, transcendentals=0, bytes_accessed=12 * planes * extent**2),
        name="convolve_planes",
    )(col, received, kernel, *tables)


def join(groups):
    n_row = groups[0][0].shape[0]
    lengths = [group[0].shape[1] for group in groups]
    n_slot = len(groups[0])
    block = n_row // 2

    def body(*refs):
        begin = 0
        for g, length in enumerate(lengths):
            for s in range(n_slot):
                refs[-1][:, s, begin : begin + length] = refs[g * n_slot + s][...]
            begin += length

    total = sum(lengths)
    return pl.pallas_call(
        body,
        grid=(n_row // block,),
        in_specs=[pl.BlockSpec((block, n, LANES), lambda i: (i, 0, 0)) for n in lengths for _ in range(n_slot)],
        out_specs=pl.BlockSpec((block, n_slot, total, LANES), lambda i: (i, 0, 0, 0)),
        out_shape=jax.ShapeDtypeStruct((n_row, n_slot, total, LANES), F32),
        name="join",
    )(*[part for group in groups for part in group])


def solution(mesh):
    n_row, n_col = mesh.shape["row"], mesh.shape["col"]
    n_dev = n_row * n_col

    def on_device(density, green_octant):
        local_x, local_y, extent = density.shape
        pairs = local_x * local_y // LANES
        freqs = extent // n_dev
        waves, even = wave_tables(extent)
        y_waves = split_table(waves)
        t_waves = split_table(waves.T)
        y_even = split_table(even)

        def by_owner(table):
            table = table.reshape(n_row, n_col, freqs, extent).transpose(1, 2, 0, 3)
            return table.reshape(n_col, freqs * n_row, extent)

        cos_z = split_table(by_owner(waves[:extent]))
        sin_z = split_table(by_owner(waves[extent:]))
        col = lax.axis_index("col").astype(jnp.int32).reshape(1)

        def exchange(value):
            value = lax.all_to_all(value.reshape(n_dev, -1, LANES), ALL, 0, 0)
            return value.reshape(n_row, n_col, -1, pairs, LANES)

        def spread(value):
            return lax.all_to_all(value.reshape(n_row, n_col, -1, LANES), "row", 0, 0)

        def send(values):
            received = []
            for s, value in enumerate(values, start=1):
                perm = [(c, (c + s) % n_col) for c in range(n_col)]
                received.append(lax.ppermute(value.reshape(n_row, -1, LANES), "col", perm))
            return received

        dens = density.reshape(-1, extent)
        green = green_octant.reshape(-1, extent)
        begin = freqs // 2
        late_rows = (begin * n_row, freqs * n_row)
        late = z_forward_slots(col, dens, sin_z, late_rows, n_row, pairs)
        late = [late[0].reshape(n_row, -1, LANES), *send(late[1:])]
        first = z_forward([(green, *y_even, 0, freqs), (dens, *y_waves, 0, freqs)], n_dev, pairs)
        first = exchange(first)
        second = z_forward([(dens, *y_waves, extent, begin)], n_dev, pairs)
        second = exchange(second)
        late = join([late])
        late = spread(late).reshape(n_row, n_col, -1, pairs, LANES)
        kernel = kernel_planes(first, freqs, y_even, extent)

        def convolve(received, relative, offset, start, stop, joined):
            return convolve_planes(
                col, received, relative, offset, kernel, start, stop - start, joined, t_waves, y_waves, extent
            )

        own, *others = convolve(first, False, freqs, 0, freqs, False)
        cos_parts = [own.reshape(n_row, -1, LANES), *send(others)]
        parts = []
        for g, (start, stop) in enumerate(((0, begin), (begin, freqs))):
            (out,) = convolve(late if g else second, bool(g), 0, start, stop, True)
            out = spread(out)
            sent = send([out[:, s] for s in range(1, n_col)])
            parts.append(([out, *sent], sin_z, (start * n_row, stop * n_row)))
        cos_b = join([cos_parts])
        cos_b = lax.all_to_all(cos_b, "row", 0, 0)
        result = z_inverse(col, parts[:1], n_row, pairs, extent, None)
        cos_part = ([cos_b], cos_z, (0, freqs * n_row))
        result = z_inverse(col, [cos_part, parts[1]], n_row, pairs, extent, result)
        return result.reshape(local_x, local_y, extent)

    spec = P("row", "col", None)
    return jax.shard_map(on_device, mesh=mesh, in_specs=(spec, spec), out_specs=spec, check_vma=False)
```

time: 332 us -> 337 us (1.015)
  starting transfers between devices: 48.5 us -> 60.5 us
  Pallas kernels: 83.9 us -> 77.3 us
    all_to_all x2, waiting for transfers between devices: 127 us -> 19.8 us  [exchange(): value = lax.all_to_all(value.reshape(n_dev, -1, LANES), ALL, 0, 0)]
    ppermute x9 -> x12, waiting for transfers between devices: 63.7 us -> 168 us  [send(): received.append(lax.ppermute(value.reshape(n_row, -1, LANES), 'col', perm))]
    pallas_call x7, Pallas kernels: 70.6 us -> 62.4 us  [the longest x3 42.5 us: convolve_planes(): pl.pallas_call(body, grid=(planes // per,), in_specs=[SCALAR, VECTOR, pl....]
    ppermute x9 -> x12, starting transfers between devices: 21.9 us -> 29.5 us  [send(): received.append(lax.ppermute(value.reshape(n_row, -1, LANES), 'col', perm))]
    all_to_all x2 -> x3, starting transfers between devices: 9.13 us -> 16.1 us  [spread(): return lax.all_to_all(value.reshape(n_row, n_col, -1, LANES), 'row', 0, 0)]
  transfers between devices with their start and end apart: 14 -> 18, of which waited for: 7 -> 10; matrix products, arithmetic and copies ran while one was open for 1% -> 1% of each run, Pallas kernels for 18% -> 20%
where the time goes in v4:
time: 337 us; the launch traced here: 333 us
  waiting for transfers between devices  189 us (56%)
  Pallas kernels  77.3 us (23%)
  starting transfers between devices  60.5 us (18%)
  local copies, waits for them, and re-layouts  6.33 us (2%)
    ppermute x12, waiting for transfers between devices, send(): received.append(lax.ppermute(value.reshape(n_row, -1, LANES), 'col', perm))  168 us
    pallas_call x3, Pallas kernels, convolve_planes(): pl.pallas_call(body, grid=(planes // per,), in_specs=[SCALAR, VECTOR, pl....  42.5 us
    ppermute x12, starting transfers between devices, send(): received.append(lax.ppermute(value.reshape(n_row, -1, LANES), 'col', perm))  29.5 us
    all_to_all x2, waiting for transfers between devices, exchange(): value = lax.all_to_all(value.reshape(n_dev, -1, LANES), ALL, 0, 0)  19.8 us
    all_to_all x3, starting transfers between devices, spread(): return lax.all_to_all(value.reshape(n_row, n_col, -1, LANES), 'row', 0, 0)  16.1 us
    all_to_all x2, starting transfers between devices, exchange(): value = lax.all_to_all(value.reshape(n_dev, -1, LANES), ALL, 0, 0)  10.4 us
    pallas_call x2, Pallas kernels, z_forward(): pl.pallas_call(body, grid=(pairs // per,), in_specs=[s for source in sour...  10.2 us
    pallas_call x2, Pallas kernels, z_inverse(): pl.pallas_call(body, grid=(pairs // per,), in_specs=specs, out_specs=line...  10 us
  transfers between devices with their start and end apart: 18, of which 10 were waited for; matrix products, arithmetic and copies ran while one was open for 1% of the time, Pallas kernels for 20%

profile of v4, /device:TPU:1, one launch (start us, length us, event | category | flops | bytes accessed | tf_op | source)
XLA Modules:
  0.0 332.8 jit_solution(6605051099539325150)
XLA Ops:
  0.0 3.6 %z_forward.3 = f32[2048,128]{1,0:T(8,128)} custom-call(f32[2048,256]{1,0:T(8,128)} %bitcast.40, bf16[512,256]{1,0:T(8,128)(2,1)} %constant.28.clone.refs_4_.yh.refs_1_, bf16[512,256]{1,0:T(8,128)(2,1)} %constant.29.clone.refs_5_.yl.refs_2_), custom_call_target="tpu_custom_call" | custom-call | flops 805306368 | bytes 4194304 | tf_op jit(solution)/shard_map/z_forward/pallas_call | solution.py:85
  3.6 7.1 %all-to-all-start.4 = ((f32[32,64,128]{2,1,0:T(8,128)}), f32[32,64,128]{2,1,0:T(8,128)S(1)}, u32[]{:S(2)}, u32[]{:S(2)}) async-start(f32[32,64,128]{2,1,0:T(8,128)} %bitcast.47), calls=%async_computation.4 | async-start | bytes 2097152 | tf_op jit(solution)/shard_map/all_to_all | solution.py:343
  10.7 6.6 %z_forward.2 = f32[8192,128]{1,0:T(8,128)} custom-call(f32[2048,256]{1,0:T(8,128)} %bitcast.48, bf16[256,256]{1,0:T(8,128)(2,1)} %constant.26.clone.refs_1_.yh, bf16[256,256]{1,0:T(8,128)(2,1)} %constant.27.clone.refs_2_.yl, f32[2048,256]{1,0:T(8,128)} %bitcast.41, bf16[512,256]{1,0:T(8,128)(2,1)} %constant.28.clone.refs_4_.yh.refs_1_, ...), custom_call_target="tpu_custom_call" | custom-call | flops 1610612736 | bytes 8388608 | tf_op jit(solution)/shard_map/z_forward/pallas_call | solution.py:85
  17.3 19.8 %all-to-all-done.4 = f32[32,64,128]{2,1,0:T(8,128)S(1)} async-done(((f32[32,64,128]{2,1,0:T(8,128)}), f32[32,64,128]{2,1,0:T(8,128)S(1)}, u32[]{:S(2)}, u32[]{:S(2)}) %all-to-all-start.4) | async-done | bytes 1048608 | tf_op jit(solution)/shard_map/all_to_all | solution.py:343
  38.0 3.3 all-to-all-start
  41.4 3.9 %z_forward_slots.1 = (f32[512,128]{1,0:T(8,128)}, f32[512,128]{1,0:T(8,128)}, f32[512,128]{1,0:T(8,128)}, f32[512,128]{1,0:T(8,128)}) custom-call(s32[1]{0:T(128)} %bitcast.col_ref, f32[2048,256]{1,0:T(8,128)} %bitcast.42, bf16[4,64,256]{2,1,0:T(8,128)(2,1)} %constant.24.clone.h_ref.refs_4_.refs_7_, bf16[4,64,256]{2,1,0:T(8,128)(2,1)} %constant.25.clone.l_ref.refs_5_.refs_8_), custom_call_target="tpu_custom_call" | custom-call | flops 402653184 | bytes 4194304 | tf_op jit(solution)/shard_map/z_forward_slots/pallas_call | solution.py:119
  46.5 2.1 collective-permute-start.4
  49.7 69.7 %collective-permute-done.3.refs_1_ = f32[8,64,128]{2,1,0:T(8,128)S(1)} collective-permute-done((f32[8,64,128]{2,1,0:T(8,128)}, f32[8,64,128]{2,1,0:T(8,128)S(1)}, u32[]{:S(2)}, u32[]{:S(2)}) %collective-permute-start.3) | collective-permute-done | bytes 262176 | tf_op jit(solution)/shard_map/ppermute | solution.py:353
  119.4 33.6 %collective-permute-done.4.refs_2_ = f32[8,64,128]{2,1,0:T(8,128)S(1)} collective-permute-done((f32[8,64,128]{2,1,0:T(8,128)}, f32[8,64,128]{2,1,0:T(8,128)S(1)}, u32[]{:S(2)}, u32[]{:S(2)}) %collective-permute-start.4) | collective-permute-done | bytes 262176 | tf_op jit(solution)/shard_map/ppermute | solution.py:353
  153.8 2.1 join.3
  155.9 5.0 %all-to-all-start.2 = ((f32[8,4,64,128]{3,2,1,0:T(8,128)}), f32[8,4,64,128]{3,2,1,0:T(8,128)S(1)}, u32[]{:S(2)}, u32[]{:S(2)}) async-start(f32[8,4,64,128]{3,2,1,0:T(8,128)} %join.3), calls=%async_computation.2 | async-start | bytes 2097152 | tf_op jit(solution)/shard_map/all_to_all | solution.py:347
  160.9 6.0 %kernel_planes.1.k_ref = f32[8,256,256]{2,1,0:T(8,128)} custom-call(f32[8,4,16,16,128]{4,3,2,1,0:T(8,128)} %bitcast.4.r_ref, bf16[256,256]{1,0:T(8,128)(2,1)} %constant.26.clone.refs_1_.yh, bf16[256,256]{1,0:T(8,128)(2,1)} %constant.27.clone.refs_2_.yl), custom_call_target="tpu_custom_call" | custom-call | flops 1610612736 | bytes 4194304 | tf_op jit(solution)/shard_map/kernel_planes/pallas_call | solution.py:231
  166.9 11.0 %convolve_planes.5 = f32[8,4,4,16,128]{4,3,2,1,0:T(8,128)} custom-call(s32[1]{0:T(128)} %bitcast.col_ref, f32[8,4,4,16,128]{4,3,2,1,0:T(8,128)} %bitcast.49, f32[8,256,256]{2,1,0:T(8,128)} %kernel_planes.1.k_ref, bf16[256,512]{1,0:T(8,128)(2,1)} %constant.30.clone.th, bf16[256,512]{1,0:T(8,128)(2,1)} %constant.31.clone.tl, ...), custom_call_target="tpu_custom_call" | custom-call | flops 4831838208 | bytes 3145728 | tf_op jit(solution)/shard_map/convolve_planes/pallas_call | solution.py:281
  177.8 4.2 %all-to-all-start.5 = ((f32[8,4,64,128]{3,2,1,0:T(8,128)}), f32[8,4,64,128]{3,2,1,0:T(8,128)S(1)}, u32[]{:S(2)}, u32[]{:S(2)}) async-start(f32[8,4,64,128]{3,2,1,0:T(8,128)} %bitcast.52), calls=%async_computation.5 | async-start | bytes 2097152 | tf_op jit(solution)/shard_map/all_to_all | solution.py:347
  182.1 11.0 %convolve_planes.4 = f32[8,4,4,16,128]{4,3,2,1,0:T(8,128)} custom-call(s32[1]{0:T(128)} %bitcast.col_ref, f32[8,4,4,16,128]{4,3,2,1,0:T(8,128)} %bitcast.51, f32[8,256,256]{2,1,0:T(8,128)} %kernel_planes.1.k_ref, bf16[256,512]{1,0:T(8,128)(2,1)} %constant.30.clone.th, bf16[256,512]{1,0:T(8,128)(2,1)} %constant.31.clone.tl, ...), custom_call_target="tpu_custom_call" | custom-call | flops 4831838208 | bytes 3145728 | tf_op jit(solution)/shard_map/convolve_planes/pallas_call | solution.py:281
  194.0 6.9 %all-to-all-start.3 = ((f32[8,4,64,128]{3,2,1,0:T(8,128)}), f32[8,4,64,128]{3,2,1,0:T(8,128)S(1)}, u32[]{:S(2)}, u32[]{:S(2)}) async-start(f32[8,4,64,128]{3,2,1,0:T(8,128)} %bitcast.50), calls=%async_computation.3 | async-start | bytes 2097152 | tf_op jit(solution)/shard_map/all_to_all | solution.py:347
  200.9 20.5 %convolve_planes.3 = (f32[8,8,16,128]{3,2,1,0:T(8,128)}, f32[8,8,16,128]{3,2,1,0:T(8,128)}, f32[8,8,16,128]{3,2,1,0:T(8,128)}, f32[8,8,16,128]{3,2,1,0:T(8,128)}) custom-call(s32[1]{0:T(128)} %bitcast.col_ref, f32[8,4,16,16,128]{4,3,2,1,0:T(8,128)} %bitcast.4.r_ref, f32[8,256,256]{2,1,0:T(8,128)} %kernel_planes.1.k_ref, bf16[256,512]{1,0:T(8,128)(2,1)} %constant.30.clone.th, ...), custom_call_target="tpu_custom_call" | custom-call | flops 9663676416 | bytes 6291456 | tf_op jit(solution)/shard_map/convolve_planes/pallas_call | solution.py:281
  221.5 5.3 %collective-permute-start = (f32[8,128,128]{2,1,0:T(8,128)}, f32[8,128,128]{2,1,0:T(8,128)S(1)}, u32[]{:S(2)}, u32[]{:S(2)}) collective-permute-start(f32[8,128,128]{2,1,0:T(8,128)} %bitcast.61), channel_id=1, source_target_pairs={{0,1},{1,2},{2,3},{3,0},{4,5},{5,6},{6,7},{7,4},{8,9},{9,10},{10,1... | collective-permute-start | bytes 1572872 | tf_op jit(solution)/shard_map/ppermute | solution.py:353
  227.2 1.7 collective-permute-start.2
  228.9 10.3 %collective-permute-done.refs_1_ = f32[8,128,128]{2,1,0:T(8,128)S(1)} collective-permute-done((f32[8,128,128]{2,1,0:T(8,128)}, f32[8,128,128]{2,1,0:T(8,128)S(1)}, u32[]{:S(2)}, u32[]{:S(2)}) %collective-permute-start) | collective-permute-done | bytes 524320 | tf_op jit(solution)/shard_map/ppermute | solution.py:353
  239.3 22.8 %collective-permute-done.1.refs_2_ = f32[8,128,128]{2,1,0:T(8,128)S(1)} collective-permute-done((f32[8,128,128]{2,1,0:T(8,128)}, f32[8,128,128]{2,1,0:T(8,128)S(1)}, u32[]{:S(2)}, u32[]{:S(2)}) %collective-permute-start.1) | collective-permute-done | bytes 524320 | tf_op jit(solution)/shard_map/ppermute | solution.py:353
  263.1 2.6 join.2
  265.7 4.4 %all-to-all-start.1 = ((f32[8,4,128,128]{3,2,1,0:T(8,128)}), f32[8,4,128,128]{3,2,1,0:T(8,128)S(1)}, u32[]{:S(2)}, u32[]{:S(2)}) async-start(f32[8,4,128,128]{3,2,1,0:T(8,128)} %join.2), calls=%async_computation.1 | async-start | bytes 4194304 | tf_op jit(solution)/shard_map/all_to_all | solution.py:384
  271.3 11.3 %collective-permute-start.9 = (f32[8,64,128]{2,1,0:T(8,128)S(1)}, f32[8,64,128]{2,1,0:T(8,128)S(1)}, u32[]{:S(2)}, u32[]{:S(2)}) collective-permute-start(f32[8,64,128]{2,1,0:T(8,128)S(1)} %get-tuple-element.23), channel_id=1, source_target_pairs={{0,1},{1,2},{2,3},{3,0},{4,5},{5,6},{6,7},{7,4},{8,9},{9,10},{10,1... | collective-permute-start | bytes 786440 | tf_op jit(solution)/shard_map/ppermute | solution.py:353
  282.5 2.1 collective-permute-start.10
  287.3 3.8 %collective-permute-done.9 = f32[8,64,128]{2,1,0:T(8,128)S(1)} collective-permute-done((f32[8,64,128]{2,1,0:T(8,128)S(1)}, f32[8,64,128]{2,1,0:T(8,128)S(1)}, u32[]{:S(2)}, u32[]{:S(2)}) %collective-permute-start.9) | collective-permute-done | bytes 262176 | tf_op jit(solution)/shard_map/ppermute | solution.py:353
  291.1 2.5 collective-permute-start.8
  293.6 9.1 %collective-permute-done.10 = f32[8,64,128]{2,1,0:T(8,128)} collective-permute-done((f32[8,64,128]{2,1,0:T(8,128)S(1)}, f32[8,64,128]{2,1,0:T(8,128)}, u32[]{:S(2)}, u32[]{:S(2)}) %collective-permute-start.10) | collective-permute-done | bytes 262176 | tf_op jit(solution)/shard_map/ppermute | solution.py:353
  302.7 3.6 %z_inverse.2.refs_9_ = f32[2048,256]{1,0:T(8,128)} custom-call(s32[1]{0:T(128)} %bitcast.col_ref, f32[2048,128]{1,0:T(8,128)} %bitcast.46, f32[512,128]{1,0:T(8,128)} %bitcast.56, f32[512,128]{1,0:T(8,128)} %bitcast.30.refs_2_, f32[512,128]{1,0:T(8,128)} %bitcast.32.refs_3_, bf16[4,64,256]{2,1,0:T(8,128)(2,1)} %constant.24.clone.h_ref.refs_4_.refs_7_, ...), custom_call_target="tpu_custom_call" | custom-call | flops 402653184 | bytes 4194304 | tf_op jit(solution)/shard_map/z_inverse/pallas_call | solution.py:173
  306.3 1.7 collective-permute-done.6
  308.0 16.9 %collective-permute-done.7 = f32[8,64,128]{2,1,0:T(8,128)S(1)} collective-permute-done((f32[8,64,128]{2,1,0:T(8,128)}, f32[8,64,128]{2,1,0:T(8,128)S(1)}, u32[]{:S(2)}, u32[]{:S(2)}) %collective-permute-start.7) | collective-permute-done | bytes 262176 | tf_op jit(solution)/shard_map/ppermute | solution.py:353
  326.4 6.4 %z_inverse.3 = f32[2048,256]{1,0:T(8,128)} custom-call(s32[1]{0:T(128)} %bitcast.col_ref, f32[4096,128]{1,0:T(8,128)} %bitcast.44, bf16[4,64,256]{2,1,0:T(8,128)(2,1)} %constant.32.clone.refs_1_, bf16[4,64,256]{2,1,0:T(8,128)(2,1)} %constant.33.clone.refs_2_, f32[2048,128]{1,0:T(8,128)} %bitcast.45, f32[512,128]{1,0:T(8,128)} %bitcast.54, ...), custom_call_target="tpu_custom_call" | custom-call | flops 1207959552 | bytes 4194304 | tf_op jit(solution)/shard_map/z_inverse/pallas_call | solution.py:173
  (47 shorter events, 11.9 us)
Async XLA Ops:
  3.6 33.4 %all-to-all-start.4 = ((f32[32,64,128]{2,1,0:T(8,128)}), f32[32,64,128]{2,1,0:T(8,128)S(1)}, u32[]{:S(2)}, u32[]{:S(2)}) async-start(f32[32,64,128]{2,1,0:T(8,128)} %bitcast.47), calls=%async_computation.4 | async-start | bytes 2097152 | tf_op jit(solution)/shard_map/all_to_all | solution.py:343
  37.0 1.0 copy-start.3
  38.0 117.9 %all-to-all-start = ((f32[32,256,128]{2,1,0:T(8,128)}), f32[32,256,128]{2,1,0:T(8,128)}, u32[]{:S(2)}, u32[]{:S(2)}) async-start(f32[32,256,128]{2,1,0:T(8,128)} %bitcast.43), calls=%async_computation | async-start | bytes 8388608 | tf_op jit(solution)/shard_map/all_to_all | solution.py:343
  45.2 74.2 %collective-permute-start.3 = (f32[8,64,128]{2,1,0:T(8,128)}, f32[8,64,128]{2,1,0:T(8,128)S(1)}, u32[]{:S(2)}, u32[]{:S(2)}) collective-permute-start(f32[8,64,128]{2,1,0:T(8,128)} %bitcast.64), channel_id=1, source_target_pairs={{0,1},{1,2},{2,3},{3,0},{4,5},{5,6},{6,7},{7,4},{8,9},{9,10},{10,1... | collective-permute-start | bytes 786440 | tf_op jit(solution)/shard_map/ppermute | solution.py:353
  46.5 106.5 %collective-permute-start.4 = (f32[8,64,128]{2,1,0:T(8,128)}, f32[8,64,128]{2,1,0:T(8,128)S(1)}, u32[]{:S(2)}, u32[]{:S(2)}) collective-permute-start(f32[8,64,128]{2,1,0:T(8,128)} %bitcast.63), channel_id=1, source_target_pairs={{0,2},{1,3},{2,0},{3,1},{4,6},{5,7},{6,4},{7,5},{8,10},{9,11},{10,... | collective-permute-start | bytes 786440 | tf_op jit(solution)/shard_map/ppermute | solution.py:353
  48.6 104.4 %collective-permute-start.5 = (f32[8,64,128]{2,1,0:T(8,128)}, f32[8,64,128]{2,1,0:T(8,128)S(1)}, u32[]{:S(2)}, u32[]{:S(2)}) collective-permute-start(f32[8,64,128]{2,1,0:T(8,128)} %bitcast.62), channel_id=1, source_target_pairs={{0,3},{1,0},{2,1},{3,2},{4,7},{5,4},{6,5},{7,6},{8,11},{9,8},{10,9... | collective-permute-start | bytes 786440 | tf_op jit(solution)/shard_map/ppermute | solution.py:353
  119.4 33.6 %copy-start.12 = (f32[8,64,128]{2,1,0:T(8,128)}, f32[8,64,128]{2,1,0:T(8,128)S(1)}, u32[]{:S(2)}) copy-start(f32[8,64,128]{2,1,0:T(8,128)S(1)} %collective-permute-done.3.refs_1_) | copy-start | bytes 786436
  153.0 0.8 copy-start.14
  155.9 21.9 %all-to-all-start.2 = ((f32[8,4,64,128]{3,2,1,0:T(8,128)}), f32[8,4,64,128]{3,2,1,0:T(8,128)S(1)}, u32[]{:S(2)}, u32[]{:S(2)}) async-start(f32[8,4,64,128]{3,2,1,0:T(8,128)} %join.3), calls=%async_computation.2 | async-start | bytes 2097152 | tf_op jit(solution)/shard_map/all_to_all | solution.py:347
  177.8 4.3 %copy-start.4 = (f32[8,4,64,128]{3,2,1,0:T(8,128)}, f32[8,4,64,128]{3,2,1,0:T(8,128)S(1)}, u32[]{:S(2)}) copy-start(f32[8,4,64,128]{3,2,1,0:T(8,128)S(1)} %all-to-all-done.2) | copy-start | bytes 3145732
  177.8 16.2 %all-to-all-start.5 = ((f32[8,4,64,128]{3,2,1,0:T(8,128)}), f32[8,4,64,128]{3,2,1,0:T(8,128)S(1)}, u32[]{:S(2)}, u32[]{:S(2)}) async-start(f32[8,4,64,128]{3,2,1,0:T(8,128)} %bitcast.52), calls=%async_computation.5 | async-start | bytes 2097152 | tf_op jit(solution)/shard_map/all_to_all | solution.py:347
  194.0 27.4 %copy-start.2 = (f32[8,4,64,128]{3,2,1,0:T(8,128)}, f32[8,4,64,128]{3,2,1,0:T(8,128)S(1)}, u32[]{:S(2)}) copy-start(f32[8,4,64,128]{3,2,1,0:T(8,128)S(1)} %all-to-all-done.5) | copy-start | bytes 3145732
  194.0 71.6 %all-to-all-start.3 = ((f32[8,4,64,128]{3,2,1,0:T(8,128)}), f32[8,4,64,128]{3,2,1,0:T(8,128)S(1)}, u32[]{:S(2)}, u32[]{:S(2)}) async-start(f32[8,4,64,128]{3,2,1,0:T(8,128)} %bitcast.50), calls=%async_computation.3 | async-start | bytes 2097152 | tf_op jit(solution)/shard_map/all_to_all | solution.py:347
  221.5 17.8 %collective-permute-start = (f32[8,128,128]{2,1,0:T(8,128)}, f32[8,128,128]{2,1,0:T(8,128)S(1)}, u32[]{:S(2)}, u32[]{:S(2)}) collective-permute-start(f32[8,128,128]{2,1,0:T(8,128)} %bitcast.61), channel_id=1, source_target_pairs={{0,1},{1,2},{2,3},{3,0},{4,5},{5,6},{6,7},{7,4},{8,9},{9,10},{10,1... | collective-permute-start | bytes 1572872 | tf_op jit(solution)/shard_map/ppermute | solution.py:353
  226.8 35.3 %collective-permute-start.1 = (f32[8,128,128]{2,1,0:T(8,128)}, f32[8,128,128]{2,1,0:T(8,128)S(1)}, u32[]{:S(2)}, u32[]{:S(2)}) collective-permute-start(f32[8,128,128]{2,1,0:T(8,128)} %bitcast.60), channel_id=1, source_target_pairs={{0,2},{1,3},{2,0},{3,1},{4,6},{5,7},{6,4},{7,5},{8,10},{9,11},{10,... | collective-permute-start | bytes 1572872 | tf_op jit(solution)/shard_map/ppermute | solution.py:353
  227.2 34.8 %collective-permute-start.2 = (f32[8,128,128]{2,1,0:T(8,128)}, f32[8,128,128]{2,1,0:T(8,128)S(1)}, u32[]{:S(2)}, u32[]{:S(2)}) collective-permute-start(f32[8,128,128]{2,1,0:T(8,128)} %bitcast.59), channel_id=1, source_target_pairs={{0,3},{1,0},{2,1},{3,2},{4,7},{5,4},{6,5},{7,6},{8,11},{9,8},{10,9... | collective-permute-start | bytes 1572872 | tf_op jit(solution)/shard_map/ppermute | solution.py:353
  239.3 22.8 %copy-start.5 = (f32[8,128,128]{2,1,0:T(8,128)}, f32[8,128,128]{2,1,0:T(8,128)S(1)}, u32[]{:S(2)}) copy-start(f32[8,128,128]{2,1,0:T(8,128)S(1)} %collective-permute-done.refs_1_) | copy-start | bytes 1572868
  262.1 0.8 copy-start.6
  262.1 1.0 copy-start.7
  265.7 19.0 %copy-start.1 = (f32[8,4,64,128]{3,2,1,0:T(8,128)}, f32[8,4,64,128]{3,2,1,0:T(8,128)S(1)}, u32[]{:S(2)}) copy-start(f32[8,4,64,128]{3,2,1,0:T(8,128)S(1)} %all-to-all-done.3) | copy-start | bytes 3145732
  265.7 59.2 %all-to-all-start.1 = ((f32[8,4,128,128]{3,2,1,0:T(8,128)}), f32[8,4,128,128]{3,2,1,0:T(8,128)S(1)}, u32[]{:S(2)}, u32[]{:S(2)}) async-start(f32[8,4,128,128]{3,2,1,0:T(8,128)} %join.2), calls=%async_computation.1 | async-start | bytes 4194304 | tf_op jit(solution)/shard_map/all_to_all | solution.py:384
  271.3 19.8 %collective-permute-start.9 = (f32[8,64,128]{2,1,0:T(8,128)S(1)}, f32[8,64,128]{2,1,0:T(8,128)S(1)}, u32[]{:S(2)}, u32[]{:S(2)}) collective-permute-start(f32[8,64,128]{2,1,0:T(8,128)S(1)} %get-tuple-element.23), channel_id=1, source_target_pairs={{0,1},{1,2},{2,3},{3,0},{4,5},{5,6},{6,7},{7,4},{8,9},{9,10},{10,1... | collective-permute-start | bytes 786440 | tf_op jit(solution)/shard_map/ppermute | solution.py:353
  282.5 20.1 %collective-permute-start.10 = (f32[8,64,128]{2,1,0:T(8,128)S(1)}, f32[8,64,128]{2,1,0:T(8,128)}, u32[]{:S(2)}, u32[]{:S(2)}) collective-permute-start(f32[8,64,128]{2,1,0:T(8,128)S(1)} %get-tuple-element.22), channel_id=1, source_target_pairs={{0,2},{1,3},{2,0},{3,1},{4,6},{5,7},{6,4},{7,5},{8,10},{9,11},{10,... | collective-permute-start | bytes 786440 | tf_op jit(solution)/shard_map/ppermute | solution.py:353
  284.6 18.1 %collective-permute-start.11 = (f32[8,64,128]{2,1,0:T(8,128)S(1)}, f32[8,64,128]{2,1,0:T(8,128)}, u32[]{:S(2)}, u32[]{:S(2)}) collective-permute-start(f32[8,64,128]{2,1,0:T(8,128)S(1)} %get-tuple-element.21), channel_id=1, source_target_pairs={{0,3},{1,0},{2,1},{3,2},{4,7},{5,4},{6,5},{7,6},{8,11},{9,8},{10,9... | collective-permute-start | bytes 786440 | tf_op jit(solution)/shard_map/ppermute | solution.py:353
  285.6 22.4 %collective-permute-start.6 = (f32[8,64,128]{2,1,0:T(8,128)}, f32[8,64,128]{2,1,0:T(8,128)S(1)}, u32[]{:S(2)}, u32[]{:S(2)}) collective-permute-start(f32[8,64,128]{2,1,0:T(8,128)} %get-tuple-element.26), channel_id=1, source_target_pairs={{0,1},{1,2},{2,3},{3,0},{4,5},{5,6},{6,7},{7,4},{8,9},{9,10},{10,1... | collective-permute-start | bytes 786440 | tf_op jit(solution)/shard_map/ppermute | solution.py:353
  287.0 37.9 %collective-permute-start.7 = (f32[8,64,128]{2,1,0:T(8,128)}, f32[8,64,128]{2,1,0:T(8,128)S(1)}, u32[]{:S(2)}, u32[]{:S(2)}) collective-permute-start(f32[8,64,128]{2,1,0:T(8,128)} %get-tuple-element.25), channel_id=1, source_target_pairs={{0,2},{1,3},{2,0},{3,1},{4,6},{5,7},{6,4},{7,5},{8,10},{9,11},{10,... | collective-permute-start | bytes 786440 | tf_op jit(solution)/shard_map/ppermute | solution.py:353
  291.1 11.6 %copy-start.10 = (f32[8,64,128]{2,1,0:T(8,128)}, f32[8,64,128]{2,1,0:T(8,128)S(1)}, u32[]{:S(2)}) copy-start(f32[8,64,128]{2,1,0:T(8,128)S(1)} %collective-permute-done.9) | copy-start | bytes 786436
  291.1 33.8 %collective-permute-start.8 = (f32[8,64,128]{2,1,0:T(8,128)}, f32[8,64,128]{2,1,0:T(8,128)S(1)}, u32[]{:S(2)}, u32[]{:S(2)}) collective-permute-start(f32[8,64,128]{2,1,0:T(8,128)} %get-tuple-element.24), channel_id=1, source_target_pairs={{0,3},{1,0},{2,1},{3,2},{4,7},{5,4},{6,5},{7,6},{8,11},{9,8},{10,9... | collective-permute-start | bytes 786440 | tf_op jit(solution)/shard_map/ppermute | solution.py:353
  308.0 17.0 %copy-start.8 = (f32[8,64,128]{2,1,0:T(8,128)}, f32[8,64,128]{2,1,0:T(8,128)S(1)}, u32[]{:S(2)}) copy-start(f32[8,64,128]{2,1,0:T(8,128)S(1)} %collective-permute-done.6) | copy-start | bytes 786436
  324.9 0.7 copy-start.9
  324.9 0.8 copy-start.11
  324.9 1.5 copy-start
  (1 other events, 0.7 us)

commit v5 on v4

--- a/solution.py
+++ b/solution.py
@@ -252,10 +252,12 @@
         for i in range(per):
             plane = read_plane(r_ref, offset + per * pl.program_id(0) + i, plane_ref.at[i], slot)
             along_x = dot(stack_left(yh[...], yl[...], 1), stack_right(*split(plane), 0), NN)
-            weight = jnp.concatenate([k_ref[i], k_ref[i]], axis=1)
             along_y = []
-            for part in (along_x[:extent], along_x[extent:]):
-                spectrum = dot(stack_left(*split(part), 1), stack_right(yh[...], yl[...], 1), NT) * weight
+            for row in range(0, 2 * extent, LANES):
+                part = along_x[row : row + LANES]
+                weight = k_ref[i, row % extent : row % extent + LANES, :]
+                weight = jnp.concatenate([weight, weight], axis=1)
+                spectrum = dot(stack_left(*split(part), 1), stack_right(th[...], tl[...], 0), NN) * weight
                 along_y.append(dot(stack_left(*split(spectrum), 1), stack_right(yh[...], yl[...], 0), NN))
             along_y = jnp.concatenate(along_y, axis=0)
             results.append(dot(stack_left(th[...], tl[...], 1), stack_right(*split(along_y), 0), NN))

time: 337 us -> 337 us (level)
  no operation moved by 1% of the time
where the time goes in v5:
time: 337 us; the launch traced here: 332 us
  waiting for transfers between devices  189 us (56%)
  Pallas kernels  76.4 us (23%)
  starting transfers between devices  60.5 us (18%)
  local copies, waits for them, and re-layouts  6.33 us (2%)
    ppermute x12, waiting for transfers between devices, send(): received.append(lax.ppermute(value.reshape(n_row, -1, LANES), 'col', perm))  168 us
    pallas_call x3, Pallas kernels, convolve_planes(): pl.pallas_call(body, grid=(planes // per,), in_specs=[SCALAR, VECTOR, pl....  41.7 us
    ppermute x12, starting transfers between devices, send(): received.append(lax.ppermute(value.reshape(n_row, -1, LANES), 'col', perm))  29.5 us
    all_to_all x2, waiting for transfers between devices, exchange(): value = lax.all_to_all(value.reshape(n_dev, -1, LANES), ALL, 0, 0)  19.8 us
    all_to_all x3, starting transfers between devices, spread(): return lax.all_to_all(value.reshape(n_row, n_col, -1, LANES), 'row', 0, 0)  16.1 us
    all_to_all x2, starting transfers between devices, exchange(): value = lax.all_to_all(value.reshape(n_dev, -1, LANES), ALL, 0, 0)  10.4 us
    pallas_call x2, Pallas kernels, z_forward(): pl.pallas_call(body, grid=(pairs // per,), in_specs=[s for source in sour...  10.2 us
    pallas_call x2, Pallas kernels, z_inverse(): pl.pallas_call(body, grid=(pairs // per,), in_specs=specs, out_specs=line...  10 us
  transfers between devices with their start and end apart: 18, of which 10 were waited for; matrix products, arithmetic and copies ran while one was open for 1% of the time, Pallas kernels for 20%

profile of v5, /device:TPU:1, one launch (start us, length us, event | category | flops | bytes accessed | tf_op | source)
XLA Modules:
  0.0 332.1 jit_solution(5198741780166707669)
XLA Ops:
  0.0 3.6 %z_forward.3 = f32[2048,128]{1,0:T(8,128)} custom-call(f32[2048,256]{1,0:T(8,128)} %bitcast.40, bf16[512,256]{1,0:T(8,128)(2,1)} %constant.28.clone.refs_4_.yh.refs_1_, bf16[512,256]{1,0:T(8,128)(2,1)} %constant.29.clone.refs_5_.yl.refs_2_), custom_call_target="tpu_custom_call" | custom-call | flops 805306368 | bytes 4194304 | tf_op jit(solution)/shard_map/z_forward/pallas_call | solution.py:85
  3.6 7.1 %all-to-all-start.4 = ((f32[32,64,128]{2,1,0:T(8,128)}), f32[32,64,128]{2,1,0:T(8,128)S(1)}, u32[]{:S(2)}, u32[]{:S(2)}) async-start(f32[32,64,128]{2,1,0:T(8,128)} %bitcast.47), calls=%async_computation.4 | async-start | bytes 2097152 | tf_op jit(solution)/shard_map/all_to_all | solution.py:345
  10.7 6.6 %z_forward.2 = f32[8192,128]{1,0:T(8,128)} custom-call(f32[2048,256]{1,0:T(8,128)} %bitcast.48, bf16[256,256]{1,0:T(8,128)(2,1)} %constant.26.clone.refs_1_.yh, bf16[256,256]{1,0:T(8,128)(2,1)} %constant.27.clone.refs_2_.yl, f32[2048,256]{1,0:T(8,128)} %bitcast.41, bf16[512,256]{1,0:T(8,128)(2,1)} %constant.28.clone.refs_4_.yh.refs_1_, ...), custom_call_target="tpu_custom_call" | custom-call | flops 1610612736 | bytes 8388608 | tf_op jit(solution)/shard_map/z_forward/pallas_call | solution.py:85
  17.3 19.8 %all-to-all-done.4 = f32[32,64,128]{2,1,0:T(8,128)S(1)} async-done(((f32[32,64,128]{2,1,0:T(8,128)}), f32[32,64,128]{2,1,0:T(8,128)S(1)}, u32[]{:S(2)}, u32[]{:S(2)}) %all-to-all-start.4) | async-done | bytes 1048608 | tf_op jit(solution)/shard_map/all_to_all | solution.py:345
  38.0 3.3 %all-to-all-start = ((f32[32,256,128]{2,1,0:T(8,128)}), f32[32,256,128]{2,1,0:T(8,128)}, u32[]{:S(2)}, u32[]{:S(2)}) async-start(f32[32,256,128]{2,1,0:T(8,128)} %bitcast.43), calls=%async_computation | async-start | bytes 8388608 | tf_op jit(solution)/shard_map/all_to_all | solution.py:345
  41.4 3.9 %z_forward_slots.1 = (f32[512,128]{1,0:T(8,128)}, f32[512,128]{1,0:T(8,128)}, f32[512,128]{1,0:T(8,128)}, f32[512,128]{1,0:T(8,128)}) custom-call(s32[1]{0:T(128)} %bitcast.col_ref, f32[2048,256]{1,0:T(8,128)} %bitcast.42, bf16[4,64,256]{2,1,0:T(8,128)(2,1)} %constant.24.clone.h_ref.refs_4_.refs_7_, bf16[4,64,256]{2,1,0:T(8,128)(2,1)} %constant.25.clone.l_ref.refs_5_.refs_8_), custom_call_target="tpu_custom_call" | custom-call | flops 402653184 | bytes 4194304 | tf_op jit(solution)/shard_map/z_forward_slots/pallas_call | solution.py:119
  46.5 2.1 collective-permute-start.4
  49.7 69.7 %collective-permute-done.3.refs_1_ = f32[8,64,128]{2,1,0:T(8,128)S(1)} collective-permute-done((f32[8,64,128]{2,1,0:T(8,128)}, f32[8,64,128]{2,1,0:T(8,128)S(1)}, u32[]{:S(2)}, u32[]{:S(2)}) %collective-permute-start.3) | collective-permute-done | bytes 262176 | tf_op jit(solution)/shard_map/ppermute | solution.py:355
  119.4 33.6 %collective-permute-done.4.refs_2_ = f32[8,64,128]{2,1,0:T(8,128)S(1)} collective-permute-done((f32[8,64,128]{2,1,0:T(8,128)}, f32[8,64,128]{2,1,0:T(8,128)S(1)}, u32[]{:S(2)}, u32[]{:S(2)}) %collective-permute-start.4) | collective-permute-done | bytes 262176 | tf_op jit(solution)/shard_map/ppermute | solution.py:355
  153.8 2.1 join.3
  155.9 5.0 %all-to-all-start.2 = ((f32[8,4,64,128]{3,2,1,0:T(8,128)}), f32[8,4,64,128]{3,2,1,0:T(8,128)S(1)}, u32[]{:S(2)}, u32[]{:S(2)}) async-start(f32[8,4,64,128]{3,2,1,0:T(8,128)} %join.3), calls=%async_computation.2 | async-start | bytes 2097152 | tf_op jit(solution)/shard_map/all_to_all | solution.py:349
  160.9 6.0 %kernel_planes.1.k_ref = f32[8,256,256]{2,1,0:T(8,128)} custom-call(f32[8,4,16,16,128]{4,3,2,1,0:T(8,128)} %bitcast.4.r_ref, bf16[256,256]{1,0:T(8,128)(2,1)} %constant.26.clone.refs_1_.yh, bf16[256,256]{1,0:T(8,128)(2,1)} %constant.27.clone.refs_2_.yl), custom_call_target="tpu_custom_call" | custom-call | flops 1610612736 | bytes 4194304 | tf_op jit(solution)/shard_map/kernel_planes/pallas_call | solution.py:231
  166.9 10.7 %convolve_planes.5 = f32[8,4,4,16,128]{4,3,2,1,0:T(8,128)} custom-call(s32[1]{0:T(128)} %bitcast.col_ref, f32[8,4,4,16,128]{4,3,2,1,0:T(8,128)} %bitcast.49, f32[8,256,256]{2,1,0:T(8,128)} %kernel_planes.1.k_ref, bf16[256,512]{1,0:T(8,128)(2,1)} %constant.30.clone.th, bf16[256,512]{1,0:T(8,128)(2,1)} %constant.31.clone.tl, ...), custom_call_target="tpu_custom_call" | custom-call | flops 4831838208 | bytes 3145728 | tf_op jit(solution)/shard_map/convolve_planes/pallas_call | solution.py:283
  177.6 4.2 %all-to-all-start.5 = ((f32[8,4,64,128]{3,2,1,0:T(8,128)}), f32[8,4,64,128]{3,2,1,0:T(8,128)S(1)}, u32[]{:S(2)}, u32[]{:S(2)}) async-start(f32[8,4,64,128]{3,2,1,0:T(8,128)} %bitcast.52), calls=%async_computation.5 | async-start | bytes 2097152 | tf_op jit(solution)/shard_map/all_to_all | solution.py:349
  181.9 10.8 %convolve_planes.4 = f32[8,4,4,16,128]{4,3,2,1,0:T(8,128)} custom-call(s32[1]{0:T(128)} %bitcast.col_ref, f32[8,4,4,16,128]{4,3,2,1,0:T(8,128)} %bitcast.51, f32[8,256,256]{2,1,0:T(8,128)} %kernel_planes.1.k_ref, bf16[256,512]{1,0:T(8,128)(2,1)} %constant.30.clone.th, bf16[256,512]{1,0:T(8,128)(2,1)} %constant.31.clone.tl, ...), custom_call_target="tpu_custom_call" | custom-call | flops 4831838208 | bytes 3145728 | tf_op jit(solution)/shard_map/convolve_planes/pallas_call | solution.py:283
  193.8 6.9 %all-to-all-start.3 = ((f32[8,4,64,128]{3,2,1,0:T(8,128)}), f32[8,4,64,128]{3,2,1,0:T(8,128)S(1)}, u32[]{:S(2)}, u32[]{:S(2)}) async-start(f32[8,4,64,128]{3,2,1,0:T(8,128)} %bitcast.50), calls=%async_computation.3 | async-start | bytes 2097152 | tf_op jit(solution)/shard_map/all_to_all | solution.py:349
  200.7 20.1 %convolve_planes.3 = (f32[8,8,16,128]{3,2,1,0:T(8,128)}, f32[8,8,16,128]{3,2,1,0:T(8,128)}, f32[8,8,16,128]{3,2,1,0:T(8,128)}, f32[8,8,16,128]{3,2,1,0:T(8,128)}) custom-call(s32[1]{0:T(128)} %bitcast.col_ref, f32[8,4,16,16,128]{4,3,2,1,0:T(8,128)} %bitcast.4.r_ref, f32[8,256,256]{2,1,0:T(8,128)} %kernel_planes.1.k_ref, bf16[256,512]{1,0:T(8,128)(2,1)} %constant.30.clone.th, ...), custom_call_target="tpu_custom_call" | custom-call | flops 9663676416 | bytes 6291456 | tf_op jit(solution)/shard_map/convolve_planes/pallas_call | solution.py:283
  220.8 5.3 %collective-permute-start = (f32[8,128,128]{2,1,0:T(8,128)}, f32[8,128,128]{2,1,0:T(8,128)S(1)}, u32[]{:S(2)}, u32[]{:S(2)}) collective-permute-start(f32[8,128,128]{2,1,0:T(8,128)} %bitcast.61), channel_id=1, source_target_pairs={{0,1},{1,2},{2,3},{3,0},{4,5},{5,6},{6,7},{7,4},{8,9},{9,10},{10,1... | collective-permute-start | bytes 1572872 | tf_op jit(solution)/shard_map/ppermute | solution.py:355
  226.6 1.7 collective-permute-start.2
  228.3 10.4 %collective-permute-done.refs_1_ = f32[8,128,128]{2,1,0:T(8,128)S(1)} collective-permute-done((f32[8,128,128]{2,1,0:T(8,128)}, f32[8,128,128]{2,1,0:T(8,128)S(1)}, u32[]{:S(2)}, u32[]{:S(2)}) %collective-permute-start) | collective-permute-done | bytes 524320 | tf_op jit(solution)/shard_map/ppermute | solution.py:355
  238.6 22.8 %collective-permute-done.1.refs_2_ = f32[8,128,128]{2,1,0:T(8,128)S(1)} collective-permute-done((f32[8,128,128]{2,1,0:T(8,128)}, f32[8,128,128]{2,1,0:T(8,128)S(1)}, u32[]{:S(2)}, u32[]{:S(2)}) %collective-permute-start.1) | collective-permute-done | bytes 524320 | tf_op jit(solution)/shard_map/ppermute | solution.py:355
  262.4 2.6 join.2
  265.0 4.4 %all-to-all-start.1 = ((f32[8,4,128,128]{3,2,1,0:T(8,128)}), f32[8,4,128,128]{3,2,1,0:T(8,128)S(1)}, u32[]{:S(2)}, u32[]{:S(2)}) async-start(f32[8,4,128,128]{3,2,1,0:T(8,128)} %join.2), calls=%async_computation.1 | async-start | bytes 4194304 | tf_op jit(solution)/shard_map/all_to_all | solution.py:386
  270.6 11.3 %collective-permute-start.9 = (f32[8,64,128]{2,1,0:T(8,128)S(1)}, f32[8,64,128]{2,1,0:T(8,128)S(1)}, u32[]{:S(2)}, u32[]{:S(2)}) collective-permute-start(f32[8,64,128]{2,1,0:T(8,128)S(1)} %get-tuple-element.23), channel_id=1, source_target_pairs={{0,1},{1,2},{2,3},{3,0},{4,5},{5,6},{6,7},{7,4},{8,9},{9,10},{10,1... | collective-permute-start | bytes 786440 | tf_op jit(solution)/shard_map/ppermute | solution.py:355
  281.9 2.0 collective-permute-start.10
  286.6 3.8 %collective-permute-done.9 = f32[8,64,128]{2,1,0:T(8,128)S(1)} collective-permute-done((f32[8,64,128]{2,1,0:T(8,128)S(1)}, f32[8,64,128]{2,1,0:T(8,128)S(1)}, u32[]{:S(2)}, u32[]{:S(2)}) %collective-permute-start.9) | collective-permute-done | bytes 262176 | tf_op jit(solution)/shard_map/ppermute | solution.py:355
  290.4 2.5 collective-permute-start.8
  292.9 9.1 %collective-permute-done.10 = f32[8,64,128]{2,1,0:T(8,128)} collective-permute-done((f32[8,64,128]{2,1,0:T(8,128)S(1)}, f32[8,64,128]{2,1,0:T(8,128)}, u32[]{:S(2)}, u32[]{:S(2)}) %collective-permute-start.10) | collective-permute-done | bytes 262176 | tf_op jit(solution)/shard_map/ppermute | solution.py:355
  302.0 3.6 %z_inverse.2.refs_9_ = f32[2048,256]{1,0:T(8,128)} custom-call(s32[1]{0:T(128)} %bitcast.col_ref, f32[2048,128]{1,0:T(8,128)} %bitcast.46, f32[512,128]{1,0:T(8,128)} %bitcast.56, f32[512,128]{1,0:T(8,128)} %bitcast.30.refs_2_, f32[512,128]{1,0:T(8,128)} %bitcast.32.refs_3_, bf16[4,64,256]{2,1,0:T(8,128)(2,1)} %constant.24.clone.h_ref.refs_4_.refs_7_, ...), custom_call_target="tpu_custom_call" | custom-call | flops 402653184 | bytes 4194304 | tf_op jit(solution)/shard_map/z_inverse/pallas_call | solution.py:173
  305.6 1.7 collective-permute-done.6
  307.3 16.9 %collective-permute-done.7 = f32[8,64,128]{2,1,0:T(8,128)S(1)} collective-permute-done((f32[8,64,128]{2,1,0:T(8,128)}, f32[8,64,128]{2,1,0:T(8,128)S(1)}, u32[]{:S(2)}, u32[]{:S(2)}) %collective-permute-start.7) | collective-permute-done | bytes 262176 | tf_op jit(solution)/shard_map/ppermute | solution.py:355
  325.7 6.4 %z_inverse.3 = f32[2048,256]{1,0:T(8,128)} custom-call(s32[1]{0:T(128)} %bitcast.col_ref, f32[4096,128]{1,0:T(8,128)} %bitcast.44, bf16[4,64,256]{2,1,0:T(8,128)(2,1)} %constant.32.clone.refs_1_, bf16[4,64,256]{2,1,0:T(8,128)(2,1)} %constant.33.clone.refs_2_, f32[2048,128]{1,0:T(8,128)} %bitcast.45, f32[512,128]{1,0:T(8,128)} %bitcast.54, ...), custom_call_target="tpu_custom_call" | custom-call | flops 1207959552 | bytes 4194304 | tf_op jit(solution)/shard_map/z_inverse/pallas_call | solution.py:173
  (47 shorter events, 12.1 us)
Async XLA Ops:
  3.6 33.4 %all-to-all-start.4 = ((f32[32,64,128]{2,1,0:T(8,128)}), f32[32,64,128]{2,1,0:T(8,128)S(1)}, u32[]{:S(2)}, u32[]{:S(2)}) async-start(f32[32,64,128]{2,1,0:T(8,128)} %bitcast.47), calls=%async_computation.4 | async-start | bytes 2097152 | tf_op jit(solution)/shard_map/all_to_all | solution.py:345
  37.0 1.0 copy-start.3
  38.0 117.9 %all-to-all-start = ((f32[32,256,128]{2,1,0:T(8,128)}), f32[32,256,128]{2,1,0:T(8,128)}, u32[]{:S(2)}, u32[]{:S(2)}) async-start(f32[32,256,128]{2,1,0:T(8,128)} %bitcast.43), calls=%async_computation | async-start | bytes 8388608 | tf_op jit(solution)/shard_map/all_to_all | solution.py:345
  45.2 74.2 %collective-permute-start.3 = (f32[8,64,128]{2,1,0:T(8,128)}, f32[8,64,128]{2,1,0:T(8,128)S(1)}, u32[]{:S(2)}, u32[]{:S(2)}) collective-permute-start(f32[8,64,128]{2,1,0:T(8,128)} %bitcast.64), channel_id=1, source_target_pairs={{0,1},{1,2},{2,3},{3,0},{4,5},{5,6},{6,7},{7,4},{8,9},{9,10},{10,1... | collective-permute-start | bytes 786440 | tf_op jit(solution)/shard_map/ppermute | solution.py:355
  46.5 106.5 %collective-permute-start.4 = (f32[8,64,128]{2,1,0:T(8,128)}, f32[8,64,128]{2,1,0:T(8,128)S(1)}, u32[]{:S(2)}, u32[]{:S(2)}) collective-permute-start(f32[8,64,128]{2,1,0:T(8,128)} %bitcast.63), channel_id=1, source_target_pairs={{0,2},{1,3},{2,0},{3,1},{4,6},{5,7},{6,4},{7,5},{8,10},{9,11},{10,... | collective-permute-start | bytes 786440 | tf_op jit(solution)/shard_map/ppermute | solution.py:355
  48.6 104.4 %collective-permute-start.5 = (f32[8,64,128]{2,1,0:T(8,128)}, f32[8,64,128]{2,1,0:T(8,128)S(1)}, u32[]{:S(2)}, u32[]{:S(2)}) collective-permute-start(f32[8,64,128]{2,1,0:T(8,128)} %bitcast.62), channel_id=1, source_target_pairs={{0,3},{1,0},{2,1},{3,2},{4,7},{5,4},{6,5},{7,6},{8,11},{9,8},{10,9... | collective-permute-start | bytes 786440 | tf_op jit(solution)/shard_map/ppermute | solution.py:355
  119.4 33.6 %copy-start.12 = (f32[8,64,128]{2,1,0:T(8,128)}, f32[8,64,128]{2,1,0:T(8,128)S(1)}, u32[]{:S(2)}) copy-start(f32[8,64,128]{2,1,0:T(8,128)S(1)} %collective-permute-done.3.refs_1_) | copy-start | bytes 786436
  153.0 0.8 copy-start.14
  155.9 21.7 %all-to-all-start.2 = ((f32[8,4,64,128]{3,2,1,0:T(8,128)}), f32[8,4,64,128]{3,2,1,0:T(8,128)S(1)}, u32[]{:S(2)}, u32[]{:S(2)}) async-start(f32[8,4,64,128]{3,2,1,0:T(8,128)} %join.3), calls=%async_computation.2 | async-start | bytes 2097152 | tf_op jit(solution)/shard_map/all_to_all | solution.py:349
  177.6 4.3 %copy-start.4 = (f32[8,4,64,128]{3,2,1,0:T(8,128)}, f32[8,4,64,128]{3,2,1,0:T(8,128)S(1)}, u32[]{:S(2)}) copy-start(f32[8,4,64,128]{3,2,1,0:T(8,128)S(1)} %all-to-all-done.2) | copy-start | bytes 3145732
  177.6 16.2 %all-to-all-start.5 = ((f32[8,4,64,128]{3,2,1,0:T(8,128)}), f32[8,4,64,128]{3,2,1,0:T(8,128)S(1)}, u32[]{:S(2)}, u32[]{:S(2)}) async-start(f32[8,4,64,128]{3,2,1,0:T(8,128)} %bitcast.52), calls=%async_computation.5 | async-start | bytes 2097152 | tf_op jit(solution)/shard_map/all_to_all | solution.py:349
  193.8 27.0 %copy-start.2 = (f32[8,4,64,128]{3,2,1,0:T(8,128)}, f32[8,4,64,128]{3,2,1,0:T(8,128)S(1)}, u32[]{:S(2)}) copy-start(f32[8,4,64,128]{3,2,1,0:T(8,128)S(1)} %all-to-all-done.5) | copy-start | bytes 3145732
  193.8 71.2 %all-to-all-start.3 = ((f32[8,4,64,128]{3,2,1,0:T(8,128)}), f32[8,4,64,128]{3,2,1,0:T(8,128)S(1)}, u32[]{:S(2)}, u32[]{:S(2)}) async-start(f32[8,4,64,128]{3,2,1,0:T(8,128)} %bitcast.50), calls=%async_computation.3 | async-start | bytes 2097152 | tf_op jit(solution)/shard_map/all_to_all | solution.py:349
  220.8 17.8 %collective-permute-start = (f32[8,128,128]{2,1,0:T(8,128)}, f32[8,128,128]{2,1,0:T(8,128)S(1)}, u32[]{:S(2)}, u32[]{:S(2)}) collective-permute-start(f32[8,128,128]{2,1,0:T(8,128)} %bitcast.61), channel_id=1, source_target_pairs={{0,1},{1,2},{2,3},{3,0},{4,5},{5,6},{6,7},{7,4},{8,9},{9,10},{10,1... | collective-permute-start | bytes 1572872 | tf_op jit(solution)/shard_map/ppermute | solution.py:355
  226.1 35.3 %collective-permute-start.1 = (f32[8,128,128]{2,1,0:T(8,128)}, f32[8,128,128]{2,1,0:T(8,128)S(1)}, u32[]{:S(2)}, u32[]{:S(2)}) collective-permute-start(f32[8,128,128]{2,1,0:T(8,128)} %bitcast.60), channel_id=1, source_target_pairs={{0,2},{1,3},{2,0},{3,1},{4,6},{5,7},{6,4},{7,5},{8,10},{9,11},{10,... | collective-permute-start | bytes 1572872 | tf_op jit(solution)/shard_map/ppermute | solution.py:355
  226.6 34.8 %collective-permute-start.2 = (f32[8,128,128]{2,1,0:T(8,128)}, f32[8,128,128]{2,1,0:T(8,128)S(1)}, u32[]{:S(2)}, u32[]{:S(2)}) collective-permute-start(f32[8,128,128]{2,1,0:T(8,128)} %bitcast.59), channel_id=1, source_target_pairs={{0,3},{1,0},{2,1},{3,2},{4,7},{5,4},{6,5},{7,6},{8,11},{9,8},{10,9... | collective-permute-start | bytes 1572872 | tf_op jit(solution)/shard_map/ppermute | solution.py:355
  238.6 22.8 %copy-start.5 = (f32[8,128,128]{2,1,0:T(8,128)}, f32[8,128,128]{2,1,0:T(8,128)S(1)}, u32[]{:S(2)}) copy-start(f32[8,128,128]{2,1,0:T(8,128)S(1)} %collective-permute-done.refs_1_) | copy-start | bytes 1572868
  261.4 0.8 copy-start.6
  261.4 1.0 copy-start.7
  265.0 19.0 %copy-start.1 = (f32[8,4,64,128]{3,2,1,0:T(8,128)}, f32[8,4,64,128]{3,2,1,0:T(8,128)S(1)}, u32[]{:S(2)}) copy-start(f32[8,4,64,128]{3,2,1,0:T(8,128)S(1)} %all-to-all-done.3) | copy-start | bytes 3145732
  265.0 59.2 %all-to-all-start.1 = ((f32[8,4,128,128]{3,2,1,0:T(8,128)}), f32[8,4,128,128]{3,2,1,0:T(8,128)S(1)}, u32[]{:S(2)}, u32[]{:S(2)}) async-start(f32[8,4,128,128]{3,2,1,0:T(8,128)} %join.2), calls=%async_computation.1 | async-start | bytes 4194304 | tf_op jit(solution)/shard_map/all_to_all | solution.py:386
  270.6 19.8 %collective-permute-start.9 = (f32[8,64,128]{2,1,0:T(8,128)S(1)}, f32[8,64,128]{2,1,0:T(8,128)S(1)}, u32[]{:S(2)}, u32[]{:S(2)}) collective-permute-start(f32[8,64,128]{2,1,0:T(8,128)S(1)} %get-tuple-element.23), channel_id=1, source_target_pairs={{0,1},{1,2},{2,3},{3,0},{4,5},{5,6},{6,7},{7,4},{8,9},{9,10},{10,1... | collective-permute-start | bytes 786440 | tf_op jit(solution)/shard_map/ppermute | solution.py:355
  281.9 20.1 %collective-permute-start.10 = (f32[8,64,128]{2,1,0:T(8,128)S(1)}, f32[8,64,128]{2,1,0:T(8,128)}, u32[]{:S(2)}, u32[]{:S(2)}) collective-permute-start(f32[8,64,128]{2,1,0:T(8,128)S(1)} %get-tuple-element.22), channel_id=1, source_target_pairs={{0,2},{1,3},{2,0},{3,1},{4,6},{5,7},{6,4},{7,5},{8,10},{9,11},{10,... | collective-permute-start | bytes 786440 | tf_op jit(solution)/shard_map/ppermute | solution.py:355
  283.9 18.1 %collective-permute-start.11 = (f32[8,64,128]{2,1,0:T(8,128)S(1)}, f32[8,64,128]{2,1,0:T(8,128)}, u32[]{:S(2)}, u32[]{:S(2)}) collective-permute-start(f32[8,64,128]{2,1,0:T(8,128)S(1)} %get-tuple-element.21), channel_id=1, source_target_pairs={{0,3},{1,0},{2,1},{3,2},{4,7},{5,4},{6,5},{7,6},{8,11},{9,8},{10,9... | collective-permute-start | bytes 786440 | tf_op jit(solution)/shard_map/ppermute | solution.py:355
  285.0 22.3 %collective-permute-start.6 = (f32[8,64,128]{2,1,0:T(8,128)}, f32[8,64,128]{2,1,0:T(8,128)S(1)}, u32[]{:S(2)}, u32[]{:S(2)}) collective-permute-start(f32[8,64,128]{2,1,0:T(8,128)} %get-tuple-element.26), channel_id=1, source_target_pairs={{0,1},{1,2},{2,3},{3,0},{4,5},{5,6},{6,7},{7,4},{8,9},{9,10},{10,1... | collective-permute-start | bytes 786440 | tf_op jit(solution)/shard_map/ppermute | solution.py:355
  286.3 37.9 %collective-permute-start.7 = (f32[8,64,128]{2,1,0:T(8,128)}, f32[8,64,128]{2,1,0:T(8,128)S(1)}, u32[]{:S(2)}, u32[]{:S(2)}) collective-permute-start(f32[8,64,128]{2,1,0:T(8,128)} %get-tuple-element.25), channel_id=1, source_target_pairs={{0,2},{1,3},{2,0},{3,1},{4,6},{5,7},{6,4},{7,5},{8,10},{9,11},{10,... | collective-permute-start | bytes 786440 | tf_op jit(solution)/shard_map/ppermute | solution.py:355
  290.4 11.6 %copy-start.10 = (f32[8,64,128]{2,1,0:T(8,128)}, f32[8,64,128]{2,1,0:T(8,128)S(1)}, u32[]{:S(2)}) copy-start(f32[8,64,128]{2,1,0:T(8,128)S(1)} %collective-permute-done.9) | copy-start | bytes 786436
  290.4 33.8 %collective-permute-start.8 = (f32[8,64,128]{2,1,0:T(8,128)}, f32[8,64,128]{2,1,0:T(8,128)S(1)}, u32[]{:S(2)}, u32[]{:S(2)}) collective-permute-start(f32[8,64,128]{2,1,0:T(8,128)} %get-tuple-element.24), channel_id=1, source_target_pairs={{0,3},{1,0},{2,1},{3,2},{4,7},{5,4},{6,5},{7,6},{8,11},{9,8},{10,9... | collective-permute-start | bytes 786440 | tf_op jit(solution)/shard_map/ppermute | solution.py:355
  307.3 17.0 %copy-start.8 = (f32[8,64,128]{2,1,0:T(8,128)}, f32[8,64,128]{2,1,0:T(8,128)S(1)}, u32[]{:S(2)}) copy-start(f32[8,64,128]{2,1,0:T(8,128)S(1)} %collective-permute-done.6) | copy-start | bytes 786436
  324.2 0.7 copy-start.9
  324.2 0.8 copy-start.11
  324.3 1.5 copy-start
  (1 other events, 0.7 us)
